TPU v7x, 256 devices: a whole 4x4x8 slice. The times are simulated.
256 devices in a mesh: dp: 8 (over z_hi, core), comp: 32 (over x, z_lo, y).
Axes of the slice: x: 4, y: 4, z: 8 (z_hi: 4, z_lo: 2; z = z_hi * 2 + z_lo), core: 2. Of those that a mesh axis runs over, the one named last changes fastest.
Arguments:
- row_ids: int32 [8192], P('dp'), may hold values from 0 to 8191
- table: float32 [8192, 1024], P('comp'), may hold values from -25 to 25, as said below
- means: float32 [16384, 1024], P('comp'), may hold values from -0.3 to 0.3
- precisions: float32 [16384, 1024], P('comp'), may hold values from 0.8 to 1.2
- mix_logits: float32 [16384], P('comp'), may hold values from -2 to 2
- step_index: int32 [1], replicated, may hold values from 0 to 65535
Outputs:
- new_means: float32 [16384, 1024], P('comp')
- new_precisions: float32 [16384, 1024], P('comp')
- new_logits: float32 [16384], P('comp')
Inputs may be any that keep to these rules, and one draw needn't show every extreme that they name: `table`: embedding rows with entries of order one and row scales that differ.
All inputs are finite; a program needn't handle non-finite values.
Results may differ from a plain program's by a relative error of at most 0.0014.
Values sent between devices are 32-bit elements; how exact they have to be, the bound alone decides.
A program may use at most 64 MiB of HBM per device.

v0:
```python
import jax
import jax.numpy as jnp
from jax import lax
from jax.sharding import PartitionSpec as P


def update(weights, means, precisions, counts, first_moment, second_moment, step_size, batch):
    retain = 1.0 - step_size
    mass_new = retain * weights + step_size * counts / batch
    prior = (retain * weights)[:, None]
    new_means = (prior * means + step_size * first_moment / batch) / mass_new[:, None]
    moved = means - new_means
    spread = (
        prior * (1.0 / precisions + moved * moved)
        + step_size
        * (second_moment - 2.0 * new_means * first_moment + new_means * new_means * counts[:, None])
        / batch
    )
    return (new_means, mass_new[:, None] / spread, jnp.log(mass_new))


def local(row_ids, table, means, precisions, mix_logits, step_index):
    highest = lax.Precision.HIGHEST
    row_count = row_ids.shape[0]
    table_rows = table.shape[0]
    local_ids = row_ids - lax.axis_index("comp") * table_rows
    inside = (local_ids >= 0) & (local_ids < table_rows)
    picked = jnp.take(table, jnp.clip(local_ids, 0, table_rows - 1), axis=0)
    samples = lax.psum(jnp.where(inside[:, None], picked, 0.0), "comp")
    squares = samples * samples
    features = jnp.concatenate([squares, samples], axis=1)
    stacked = jnp.concatenate([precisions, -2.0 * precisions * means], axis=1)
    offset = (
        mix_logits
        + 0.5 * jnp.sum(jnp.log(precisions), axis=1)
        - 0.5 * jnp.sum(precisions * means * means, axis=1)
    )
    quadratic = lax.dot_general(
        features,
        stacked,
        (((1,), (1,)), ((), ())),
        precision=highest,
        preferred_element_type=jnp.float32,
    )
    scores = offset[None, :] - 0.5 * quadratic
    local_top = jnp.max(scores, axis=1)
    logit_top = jnp.max(mix_logits, keepdims=True)
    peak_rows, peak_logit = lax.pmax((local_top, logit_top), "comp")
    row_mass = jnp.sum(jnp.exp(scores - peak_rows[:, None]), axis=1)
    logit_mass = jnp.sum(jnp.exp(mix_logits - peak_logit), keepdims=True)
    total_rows, total_logit = lax.psum((row_mass, logit_mass), "comp")
    resp = jnp.exp(scores - peak_rows[:, None]) / total_rows[:, None]
    weights = jnp.exp(mix_logits - peak_logit) / total_logit
    counts = jnp.sum(resp, axis=0)
    first_moment = lax.dot_general(
        resp,
        samples,
        (((0,), (0,)), ((), ())),
        precision=highest,
        preferred_element_type=jnp.float32,
    )
    second_moment = lax.dot_general(
        resp,
        squares,
        (((0,), (0,)), ((), ())),
        precision=highest,
        preferred_element_type=jnp.float32,
    )
    step_size = (2.0 + step_index[0].astype(jnp.float32) / 8192.0) ** (-0.6)
    batch_rows = 1.0 * row_count * lax.axis_size("dp")
    counts, first_moment, second_moment = lax.psum((counts, first_moment, second_moment), "dp")
    new_means, new_precisions, new_logits = update(
        weights, means, precisions, counts, first_moment, second_moment, step_size, batch_rows
    )
    return (new_means, new_precisions, new_logits)


def solution(mesh):
    placed = (P("dp"), P("comp", None), P("comp", None), P("comp", None), P("comp"), P())
    return jax.shard_map(
        local,
        mesh=mesh,
        in_specs=placed,
        out_specs=(P("comp", None), P("comp", None), P("comp")),
        check_vma=False,
    )
```

profile of v0, /device:TPU:33, one launch (start us, length us, event | category | flops | bytes accessed | tf_op | source)
XLA Modules:
  0.0 678.9 jit_solution(12425040569259973315)
XLA Ops:
  7.2 0.0 all-reduce.6.cloned.1.call-start
  7.2 0.8 compare_and_fusion.1
  8.0 0.7 fusion.11
  8.7 5.4 gather_fusion
  14.1 4.1 select_select_fusion
  18.3 0.0 all-reduce.8.cloned.1.call-start
  18.4 1.5 copy-done.3
  19.9 3.5 log_reduce_fusion
  23.4 0.6 fusion.21
  24.0 295.1 %all-reduce.6.cloned.1.call-done = f32[1024,1024]{1,0:T(8,128)} async-done(((f32[1024,1024]{1,0:T(8,128)}), f32[1024,1024]{1,0:T(8,128)}) %all-reduce.6.cloned.1.call-update) | async-done | bytes 4194320 | tf_op jit(solution)/shard_map/psum | solution.py:29
  319.0 5.0 mul.104
  324.0 0.3 copy-done.5
  324.4 14.8 %fusion.8 = (f32[1024]{0:T(1024)S(1)}, f32[1024,512]{0,1:T(8,128)}) fusion(f32[512]{0:T(512)S(1)} %get-tuple-element.20, f32[512,1024]{1,0:T(8,128)S(1)} %copy-done.5, f32[512,1024]{1,0:T(8,128)S(1)} %copy-done.3, f32[1024,1024]{1,0:T(8,128)S(1)} %copy-done.1, f32[1024,1024]{1,0:T(8,128)S(1)} %mul.104), kind=kOutput, calls=%fused_computation.17 | convolution fusion | flops 12889619456 | bytes 14686208 | tf_op jit(solution)/shard_map/dot_general | solution.py:38
  339.2 67.5 %all-reduce.1 = (f32[1024]{0:T(1024)S(1)}, f32[]{:T(128)}) all-reduce(f32[1024]{0:T(1024)S(1)} %get-tuple-element.21, f32[]{:T(128)} %get-tuple-element.19), channel_id=1, replica_groups=mesh['dp'=8,'comp'=32] {'comp'}, use_global_device_ids=true, to_apply=%region_8.9 | all-reduce | flops 1025 | bytes 8200 | tf_op jit(solution)/shard_map/pmax | solution.py:48
  406.7 1.2 fusion.12
  407.8 2.1 fusion.10
  409.9 65.0 %all-reduce = (f32[1024]{0:T(1024)S(1)}, f32[]{:T(128)}) all-reduce(f32[1024]{0:T(1024)S(1)} %fusion.10, f32[]{:T(128)} %fusion.12), channel_id=1, replica_groups=mesh['dp'=8,'comp'=32] {'comp'}, use_global_device_ids=true, to_apply=%region_10.11 | all-reduce | flops 1025 | bytes 8200 | tf_op jit(solution)/shard_map/psum | solution.py:51
  475.0 11.3 %fusion.14 = f32[512,1024]{1,0:T(8,128)} fusion(f32[1024,1024]{1,0:T(8,128)} %all-reduce.6.cloned.1.call-done, f32[1024,512]{0,1:T(8,128)} %get-tuple-element.22, f32[1024]{0:T(1024)S(1)} %get-tuple-element.5, f32[1024]{0:T(1024)S(1)} %get-tuple-element.7, f32[512]{0:T(512)S(1)} %get-tuple-element.20), kind=kOutput, calls=%fused_computation.30 | convolution fusion | flops 6445596672 | bytes 8398848 | tf_op jit(solution)/shard_map/dot_general | solution.py:62
  486.2 8.6 %fusion.18 = f32[512,1024]{1,0:T(8,128)} fusion(f32[1024,1024]{1,0:T(8,128)S(1)} %copy-done.2, f32[1024,512]{0,1:T(8,128)S(1)} %copy-done.4, f32[1024]{0:T(1024)S(1)} %get-tuple-element.5, f32[1024]{0:T(1024)S(1)} %get-tuple-element.7, f32[512]{0:T(512)S(1)} %get-tuple-element.20), kind=kOutput, calls=%fused_computation.33 | convolution fusion | flops 6444548096 | bytes 8398848 | tf_op jit(solution)/shard_map/dot_general | solution.py:55
  495.5 2.2 fusion.17
  497.8 63.7 %psum.46 = f32[512]{0:T(512)S(1)} all-reduce(f32[512]{0:T(512)S(1)} %fusion.17), channel_id=1, replica_groups=mesh['dp'=8,'comp'=32] {'dp'}, use_global_device_ids=true, to_apply=%region_13.14 | all-reduce | flops 512 | bytes 4096 | tf_op jit(solution)/shard_map/psum | solution.py:71
  561.5 1.8 fusion.20
  563.3 103.8 %all-reduce.8.cloned.1.call-done = (f32[512,1024]{1,0:T(8,128)}, f32[512,1024]{1,0:T(8,128)}) async-done(((f32[512,1024]{1,0:T(8,128)}, f32[512,1024]{1,0:T(8,128)}), (f32[512,1024]{1,0:T(8,128)}, f32[512,1024]{1,0:T(8,128)})) %all-reduce.8.cloned.1.call-update) | async-done | bytes 4194320 | tf_op jit(solution)/shard_map/psum | solution.py:71
  667.1 5.0 add_divide_fusion
  (14 shorter events, 0.1 us)
Async XLA Ops:
  7.2 1.5 copy-start
  7.2 311.9 %all-reduce.6.cloned.1.call-start = ((), (), s32[]{:S(2)}) async-start(), calls=%async_computation | async-start | bytes 8388608 | tf_op jit(solution)/shard_map/psum | solution.py:29
  18.3 1.6 copy-start.3
  18.3 5.1 copy-start.6
  18.3 648.8 %all-reduce.8.cloned.1.call-start = ((), (), s32[]{:S(2)}) async-start(), calls=%async_computation.1 | async-start | bytes 8388608 | tf_op jit(solution)/shard_map/psum | solution.py:71
  319.0 5.0 copy-start.1
  319.0 5.3 copy-start.5
  475.0 11.3 %copy-start.2 = (f32[1024,1024]{1,0:T(8,128)S(1)}, f32[1024,1024]{1,0:T(8,128)}, u32[]{:S(2)}) copy-start(f32[1024,1024]{1,0:T(8,128)} %all-reduce.6.cloned.1.call-done) | copy-start | bytes 12582916
  475.0 11.3 %copy-start.4 = (f32[1024,512]{0,1:T(8,128)S(1)}, f32[1024,512]{0,1:T(8,128)}, u32[]{:S(2)}) copy-start(f32[1024,512]{0,1:T(8,128)} %get-tuple-element.22) | copy-start | bytes 6291460
Sparse Core Ops, SparseCore 0:
  18.4 300.5 all-reduce.5
  494.9 172.0 all-reduce.7
where the time goes:
time: 683 us; the launch traced here: 679 us
  waiting for transfers between devices  399 us (58%)
  blocking collectives  196 us (29%)
  matrix products  34.7 us (5%)
  other arithmetic  26.9 us (4%)
  between operations  14.8 us (2%)
  local copies, waits for them, and re-layouts  7.31 us (1%)
    psum x1, waiting for transfers between devices, local(): samples = lax.psum(jnp.where(inside[:, None], picked, 0.0), 'comp')  295 us
    psum x1, waiting for transfers between devices, local(): lax.psum((counts, first_moment, second_moment), 'dp')  104 us
    pmax x1, blocking collectives, local(): peak_rows, peak_logit = lax.pmax((local_top, logit_top), 'comp')  67.5 us
    psum x1, blocking collectives, local(): total_rows, total_logit = lax.psum((row_mass, logit_mass), 'comp')  65 us
    psum x1, blocking collectives, local(): lax.psum((counts, first_moment, second_moment), 'dp')  63.7 us
    dot_general x1, matrix products, local(): lax.dot_general(features, stacked, (((1,), (1,)), ((), ())), precision=hi...  14.8 us
  transfers between devices with their start and end apart: 2, of which 2 were waited for; matrix products, arithmetic and copies ran while one was open for 1% of the time, Pallas kernels for 0%

commit v1 on v0

v1 whole, which is shorter than its diff:
```python
import jax
import jax.numpy as jnp
from jax import lax
from jax.sharding import PartitionSpec as P


def split(value):
    high = lax.reduce_precision(value, 8, 7)
    return high.astype(jnp.bfloat16), (value - high).astype(jnp.bfloat16)


def product(left, right, dims):
    def one(a, b):
        return lax.dot_general(a, b, (dims, ((), ())), preferred_element_type=jnp.float32)

    return one(left[0], right[0]) + (one(left[0], right[1]) + one(left[1], right[0]))


def multiplicity(ids, part, parts, owners, share):
    per_owner = parts * share
    owner = ids // per_owner
    within = ids % per_owner
    mine = (within // share) == part
    row = within % share
    left = (owner[None, :] == lax.broadcasted_iota(jnp.int32, (owners, 1), 0)) & mine[None, :]
    right = row[None, :] == lax.broadcasted_iota(jnp.int32, (share, 1), 0)
    found = lax.dot_general(
        left.astype(jnp.bfloat16),
        right.astype(jnp.bfloat16),
        (((1,), (1,)), ((), ())),
        preferred_element_type=jnp.float32,
    )
    return found.reshape(-1)


def local(row_ids, table, means, precisions, mix_logits, step_index):
    dp, comp = lax.axis_size("dp"), lax.axis_size("comp")
    part = lax.axis_index("dp")
    share = table.shape[0] // dp
    batch = 1.0 * row_ids.shape[0] * dp
    ids = lax.all_gather(row_ids, "dp", tiled=True)
    mine = lax.dynamic_slice_in_dim(table, part * share, share, 0)
    samples = lax.all_gather(mine, "comp", tiled=True)
    times = multiplicity(ids, part, dp, comp, share)

    squares = samples * samples
    s, q = split(samples), split(squares)
    excess = precisions - 1.0
    cross = -2.0 * precisions * means
    e, c = split(excess), split(cross)
    offset = (
        mix_logits
        + 0.5 * jnp.sum(jnp.log(precisions), axis=1)
        - 0.5 * jnp.sum(precisions * means * means, axis=1)
    )
    lanes = ((1,), (1,))
    quadratic = product(e, q, lanes) + product(c, s, lanes)
    scores = offset[:, None] - 0.5 * quadratic
    top = jnp.max(scores, axis=0)
    raised = jnp.exp(scores - top[None, :])
    mass = jnp.sum(raised, axis=0)
    logit_top = jnp.max(mix_logits)
    logit_raised = jnp.exp(mix_logits - logit_top)
    logit_mass = jnp.sum(logit_raised)
    packed = jnp.concatenate([top, mass, jnp.full((128,), logit_top), jnp.full((128,), logit_mass)])
    every = lax.all_gather(packed, "comp")
    rows = top.shape[0]
    tops, masses = every[:, :rows], every[:, rows : 2 * rows]
    peak = jnp.max(tops, axis=0)
    total = jnp.sum(masses * jnp.exp(tops - peak[None, :]), axis=0)
    factor = jnp.exp(top - peak) / total * times
    resp = raised * factor[None, :]
    logit_tops, logit_masses = every[:, 2 * rows], every[:, 2 * rows + 128]
    logit_peak = jnp.max(logit_tops)
    logit_total = jnp.sum(logit_masses * jnp.exp(logit_tops - logit_peak))
    weights = logit_raised * (jnp.exp(logit_top - logit_peak) / logit_total)

    counts = jnp.sum(resp, axis=1)
    r = split(resp)
    inner = ((1,), (0,))
    first = product(r, s, inner)
    second = product(r, q, inner)
    first, second = (lax.psum_scatter(x, "dp", scatter_dimension=0, tiled=True) for x in (first, second))
    counts = lax.psum(counts, "dp")

    def own(x):
        size = x.shape[0] // dp
        return lax.dynamic_slice_in_dim(x, part * size, size, 0)

    step = (2.0 + step_index[0].astype(jnp.float32) / 8192.0) ** (-0.6)
    retain = 1.0 - step
    mass_all = retain * weights + step * counts / batch
    new_logits = jnp.log(mass_all)
    mass_new = own(mass_all)[:, None]
    prior = own(retain * weights)[:, None]
    own_counts = own(counts)[:, None]
    own_means = own(means)
    new_means = (prior * own_means + step * first / batch) / mass_new
    moved = own_means - new_means
    spread = (
        prior * (1.0 / own(precisions) + moved * moved)
        + step * (second - 2.0 * new_means * first + new_means * new_means * own_counts) / batch
    )
    new_precisions = mass_new / spread
    new_means, new_precisions = (lax.all_gather(x, "dp", tiled=True) for x in (new_means, new_precisions))
    return new_means, new_precisions, new_logits


def solution(mesh):
    placed = (P("dp"), P("comp", None), P("comp", None), P("comp", None), P("comp"), P())
    return jax.shard_map(
        local,
        mesh=mesh,
        in_specs=placed,
        out_specs=(P("comp", None), P("comp", None), P("comp")),
        check_vma=False,
    )
```

time: 683 us -> 448 us (0.66)
  waiting for transfers between devices: 399 us -> 250 us
  blocking collectives: 196 us -> 133 us
  matrix products: 34.7 us -> 21.1 us
  other arithmetic: 26.9 us -> 15.3 us
    psum x2 -> x0, waiting for transfers between devices: 399 us -> none  [the longest x1 295 us: local(): samples = lax.psum(jnp.where(inside[:, None], picked, 0.0), 'comp')]
    all_gather x0 -> x3, waiting for transfers between devices: none -> 187 us  [the longest x1 113 us: local(): samples = lax.all_gather(mine, 'comp', tiled=True)]
    all_gather x0 -> x2, blocking collectives: none -> 83.6 us  [the longest x1 65.6 us: local(): every = lax.all_gather(packed, 'comp')]
    psum x2 -> x1, blocking collectives: 129 us -> 49 us  [local(): counts = lax.psum(counts, 'dp')]
    pmax x1 -> x0, blocking collectives: 67.5 us -> none  [local(): peak_rows, peak_logit = lax.pmax((local_top, logit_top), 'comp')]
    reduce_scatter x0 -> x2, waiting for transfers between devices: none -> 62.3 us  [local(): lax.psum_scatter(x, 'dp', scatter_dimension=0, tiled=True)]
    dot_general x3 -> x13, matrix products: 34.7 us -> 21.1 us  [the longest x12 20.6 us: one(): lax.dot_general(a, b, (dims, ((), ())), preferred_element_type=jnp.float32)]
  transfers between devices with their start and end apart: 2 -> 5, of which waited for: 2 -> 5; matrix products, arithmetic and copies ran while one was open for 1% -> 4% of each run, Pallas kernels for 0% -> 0%
where the time goes in v1:
time: 448 us; the launch traced here: 445 us
  waiting for transfers between devices  250 us (56%)
  blocking collectives  133 us (30%)
  matrix products  21.1 us (5%)
  between operations  16.7 us (4%)
  other arithmetic  15.3 us (3%)
  local copies, waits for them, and re-layouts  10.1 us (2%)
    all_gather x1, waiting for transfers between devices, local(): samples = lax.all_gather(mine, 'comp', tiled=True)  113 us
    all_gather x2, waiting for transfers between devices, local(): lax.all_gather(x, 'dp', tiled=True)  73.5 us
    all_gather x1, blocking collectives, local(): every = lax.all_gather(packed, 'comp')  65.6 us
    reduce_scatter x2, waiting for transfers between devices, local(): lax.psum_scatter(x, 'dp', scatter_dimension=0, tiled=True)  62.3 us
    psum x1, blocking collectives, local(): counts = lax.psum(counts, 'dp')  49 us
    dot_general x12, matrix products, one(): lax.dot_general(a, b, (dims, ((), ())), preferred_element_type=jnp.float32)  20.6 us
    all_gather x1, blocking collectives, local(): ids = lax.all_gather(row_ids, 'dp', tiled=True)  18 us
  transfers between devices with their start and end apart: 5, of which 5 were waited for; matrix products, arithmetic and copies ran while one was open for 4% of the time, Pallas kernels for 0%

profile of v1, /device:TPU:33, one launch (start us, length us, event | category | flops | bytes accessed | tf_op | source)
XLA Modules:
  0.0 445.5 jit_solution(17200917461490478965)
XLA Ops:
  9.1 18.0 %all_gather.21 = s32[8192]{0:T(1024)S(1)} all-gather(s32[1024]{0:T(1024)} %param.6), channel_id=1, replica_groups=mesh['dp'=8,'comp'=32] {'dp'}, dimensions={0}, use_global_device_ids=true | all-gather | bytes 36864 | tf_op jit(solution)/shard_map/all_gather | solution.py:41
  29.0 3.9 log_reduce_fusion
  34.0 113.1 %all-gather.6.cloned.1.call-done = f32[1024,1024]{1,0:T(8,128)} async-done(((f32[32,1024]{1,0:T(8,128)}), f32[1024,1024]{1,0:T(8,128)}) %all-gather.6.cloned.1.call-update) | async-done | bytes 4194320 | tf_op jit(solution)/shard_map/all_gather | solution.py:43
  147.1 2.9 reduce-precision_convert_fusion.1
  150.0 1.3 fusion.10
  151.4 1.3 fusion.27
  152.7 1.3 fusion.44
  154.9 1.3 fusion.18
  156.2 1.4 fusion.25
  158.4 1.7 fusion.43
  161.7 65.6 %all-gather.1 = f32[32,1,2304]{2,1,0:T(1,128)S(1)} all-gather(f32[1,1,2304]{2,1,0:T(1,128)S(1)} %reshape.45), channel_id=2, replica_groups=mesh['dp'=8,'comp'=32] {'comp'}, dimensions={0}, use_global_device_ids=true | all-gather | bytes 304128 | tf_op jit(solution)/shard_map/all_gather | solution.py:66
  229.1 1.3 fusion.16
  230.4 2.6 add_add_fusion.1
  233.1 3.3 fusion.46
  236.5 1.3 fusion.23
  238.1 2.6 add_add_fusion
  245.3 49.0 %psum.7 = f32[512]{0:T(512)S(1)} all-reduce(f32[512]{0:T(512)S(1)} %get-tuple-element.13), channel_id=1, replica_groups=mesh['dp'=8,'comp'=32] {'dp'}, use_global_device_ids=true, to_apply=%region_12.13 | all-reduce | flops 512 | bytes 4096 | tf_op jit(solution)/shard_map/psum | solution.py:84
  295.7 16.3 %reduce-scatter.3.cloned.1.call-done = f32[64,1024]{1,0:T(8,128)} async-done(((f32[512,1024]{1,0:T(8,128)}), f32[64,1024]{1,0:T(8,128)}) %reduce-scatter.3.cloned.1.call-update) | async-done | bytes 262160 | tf_op jit(solution)/shard_map/reduce_scatter | solution.py:83
  312.0 46.0 %reduce-scatter.5.cloned.1.call-done = f32[64,1024]{1,0:T(8,128)} async-done(((f32[512,1024]{1,0:T(8,128)}), f32[64,1024]{1,0:T(8,128)}) %reduce-scatter.5.cloned.1.call-update) | async-done | bytes 262160 | tf_op jit(solution)/shard_map/reduce_scatter | solution.py:83
  358.0 2.2 add_divide_fusion
  360.8 37.1 %all-gather.8.cloned.1.call-done = f32[512,1024]{1,0:T(8,128)} async-done(((f32[64,1024]{1,0:T(8,128)}), f32[512,1024]{1,0:T(8,128)}) %all-gather.8.cloned.1.call-update) | async-done | bytes 2097168 | tf_op jit(solution)/shard_map/all_gather | solution.py:105
  397.9 36.4 %all-gather.10.cloned.1.call-done = f32[512,1024]{1,0:T(8,128)} async-done(((f32[64,1024]{1,0:T(8,128)}), f32[512,1024]{1,0:T(8,128)}) %all-gather.10.cloned.1.call-update) | async-done | bytes 2097168 | tf_op jit(solution)/shard_map/all_gather | solution.py:105
  434.3 3.3 copy.15
  437.6 1.3 copy.16
  (60 shorter events, 14.4 us)
Async XLA Ops:
  7.2 1.2 copy-start
  7.2 139.9 %all-gather.6.cloned.1.call-start = ((), (), s32[]{:S(2)}) async-start(), calls=%async_computation.2 | async-start | bytes 4325376 | tf_op jit(solution)/shard_map/all_gather | solution.py:43
  9.1 302.9 %reduce-scatter.3.cloned.1.call-start = ((), (), s32[]{:S(2)}) async-start(), calls=%async_computation.3 | async-start | bytes 2359296 | tf_op jit(solution)/shard_map/reduce_scatter | solution.py:83
  29.0 3.9 copy-start.12
  34.0 116.0 %copy-start.1 = (f32[512,1024]{1,0:T(8,128)S(1)}, f32[512,1024]{1,0:T(8,128)}, u32[]{:S(2)}) copy-start(f32[512,1024]{1,0:T(8,128)} %param.9) | copy-start | bytes 6291460
  150.0 1.3 copy-start.7
  151.3 1.3 copy-start.11
  152.7 2.2 copy-start.4
  156.2 1.6 copy-start.2
  156.2 2.2 copy-start.3
  227.8 1.3 copy-start.9
  233.1 125.0 %reduce-scatter.5.cloned.1.call-start = ((), (), s32[]{:S(2)}) async-start(), calls=%async_computation.5 | async-start | bytes 2359296 | tf_op jit(solution)/shard_map/reduce_scatter | solution.py:83
  233.1 3.3 copy-start.5
  233.1 3.4 copy-start.10
  236.5 1.6 copy-start.8
  240.8 157.1 %all-gather.8.cloned.1.call-start = ((), (), s32[]{:S(2)}) async-start(), calls=%async_computation.4 | async-start | bytes 2359296 | tf_op jit(solution)/shard_map/all_gather | solution.py:105
  360.2 74.1 %all-gather.10.cloned.1.call-start = ((), (), s32[]{:S(2)}) async-start(), calls=%async_computation.6 | async-start | bytes 2359296 | tf_op jit(solution)/shard_map/all_gather | solution.py:105
  434.3 3.3 copy-start.6
Sparse Core Ops, SparseCore 0:
  10.4 136.6 all-gather.5
  233.2 78.7 reduce-scatter.2
  315.1 42.8 reduce-scatter.4
  360.4 37.4 all-gather.7
  400.2 34.0 all-gather.9

commit v2 on v0

v2 whole, which is shorter than its diff:
```python
import functools

import jax
import jax.numpy as jnp
from jax import lax
from jax.experimental import pallas as pl
from jax.experimental.pallas import tpu as pltpu
from jax.sharding import PartitionSpec as P

F32, BF16 = jnp.float32, jnp.bfloat16
NX, NZ, NY = 4, 2, 4
NH, NC = 4, 2
LANES = (((1,), (1,)), ((), ()))
INNER = (((1,), (0,)), ((), ()))


def split(value):
    high = value.astype(BF16)
    return high, (value - high.astype(F32)).astype(BF16)


def mul(left, right, dims, precision=None):
    return lax.dot_general(left, right, dims, precision=precision, preferred_element_type=F32)


class Copy:
    def __init__(self, src, dst, send_sem, recv_sem, to):
        self.make = lambda: pltpu.make_async_remote_copy(
            src_ref=src, dst_ref=dst, send_sem=send_sem, recv_sem=recv_sem, device_id={"dp": to}
        )

    def start(self):
        self.make().start()

    def wait_send(self):
        self.make().wait_send()

    def wait_recv(self):
        self.make().wait_recv()


def kernel(
    ids_ref, table_ref, means_ref, prec_ref, logits_ref, step_ref,
    out_m, out_p, out_l,
    rows, ids_all, a_hi, a_lo, f_hi, f_lo, score, r_hi, r_lo, offset, tops, times_ref,
    xb, yb, zb, counts_all, columns,
    sib_out, sib_in, part, from_r, from_l, own_r, own_l,
    local_sem, ids_send, ids_recv, row_send, row_recv, xs, xr, ys, yr, zs, zr, cs, cr,
    sib_s, sib_r, opp_s, opp_r, dir_s, dir_r, acc_s, acc_r,
    gz_s, gz_r, gf_s, gs_s, gs_r,
):
    dp, comp = lax.axis_index("dp"), lax.axis_index("comp")
    h, core = dp // NC, dp % NC
    x, zl, y = comp // (NZ * NY), (comp // NY) % NZ, comp % NY
    n_dp = NH * NC
    share = rows.shape[1]
    half = share // 2
    comps, width = means_ref.shape
    n_rows = f_hi.shape[0]

    def at(dx, dz, dy):
        return ((x + dx) % NX) * (NZ * NY) + ((zl + dz) % NZ) * NY + (y + dy) % NY

    def dp_at(dh, dc):
        return ((h + dh) % NH) * NC + (core + dc) % NC

    peers_c = [at(d, 0, 0) for d in (1, 2, 3)] + [at(0, 0, d) for d in (1, 2, 3)] + [at(0, 1, 0)]
    peers_d = [dp_at(a, b) for a in range(NH) for b in range(NC) if (a, b) != (0, 0)]
    barrier = pltpu.get_barrier_semaphore()
    for peer in peers_c:
        pl.semaphore_signal(barrier, inc=1, device_id={"comp": peer})
    for peer in peers_d:
        pl.semaphore_signal(barrier, inc=1, device_id={"dp": peer})
    pl.semaphore_wait(barrier, len(peers_c) + len(peers_d))

    waits = []

    def send(src, dst, send_sem, recv_sem, **where):
        copy = pltpu.make_async_remote_copy(
            src_ref=src, dst_ref=dst, send_sem=send_sem, recv_sem=recv_sem, device_id=where
        )
        copy.start()
        return copy

    me = at(0, 0, 0)
    mine = pltpu.make_async_copy(table_ref.at[pl.ds(dp * share, share)], rows.at[me], local_sem.at[0])
    mine.start()
    sends = [0]

    def piece(ref, slot, b):
        return ref.at[slot, pl.ds(b * half, half)]

    def push(slot, b, dx, dz, dy, source=None):
        src = piece(rows, slot, b) if source is None else source
        k = sends[0]
        sends[0] += 1
        waits.append(
            send(src, piece(rows, slot, b), row_send.at[k], row_recv.at[slot, b], comp=at(dx, dz, dy))
        )

    def arrived(slot, b):
        pltpu.make_async_copy(piece(rows, slot, b), piece(rows, slot, b), row_recv.at[slot, b]).wait()

    def own(b):
        return table_ref.at[pl.ds(dp * share + b * half, half)]

    for b in (0, 1):
        push(me, b, 0, 1, 0, own(b))
    first = [(1, 0, 0), (-1, 0, 0)], [(0, 0, 1), (0, 0, -1)]
    for b in (0, 1):
        for to in first[b]:
            push(me, b, *to, own(b))
    for b in (0, 1):
        for to in first[1 - b]:
            push(me, b, *to, own(b))
    ids_copies = [
        send(ids_ref, ids_all.at[dp], ids_send.at[k], ids_recv.at[dp], dp=peer)
        for k, peer in enumerate(peers_d)
    ]
    ids_all[dp] = ids_ref[...]

    row_block = 32

    def factors(i, carry):
        at_rows = pl.ds(pl.multiple_of(i * row_block, row_block), row_block)
        p, m = prec_ref[at_rows, :], means_ref[at_rows, :]
        cross = p * m
        hi, lo = split(cross)
        a_hi[at_rows, :width], a_lo[at_rows, :width] = hi, lo
        hi, lo = split(-0.5 * (p - 1.0))
        a_hi[at_rows, width:], a_lo[at_rows, width:] = hi, lo
        offset[at_rows, :] = 0.5 * jnp.sum(jnp.log(p) - cross * m, axis=1, keepdims=True)
        return carry

    for b in (0, 1):
        arrived(at(0, 1, 0), b)
        for to in first[b] + first[1 - b]:
            push(at(0, 1, 0), b, *to)
    lax.fori_loop(0, comps // row_block, factors, 0)
    logits = logits_ref[...]
    turned = jnp.transpose(jnp.broadcast_to(logits, (8, comps)))
    offset[...] = offset[...] + turned[:, 0:1]

    def vec(d, b):
        return (d, 0) if b == 0 else (0, d)

    for rel in (0, 1):
        for b in (0, 1):
            for d in (-1, 1):
                dx, dy = vec(d, b)
                slot = at(dx, rel, dy)
                arrived(slot, b)
                if (rel == 0) == (d == -1):
                    fx, fy = vec(-d, b)
                    push(slot, b, fx, 0, fy)
                for to in first[1 - b]:
                    push(slot, b, *to)
    for rel in (0, 1):
        for b in (0, 1):
            dx, dy = vec(2, b)
            slot = at(dx, rel, dy)
            arrived(slot, b)
            for to in first[1 - b]:
                push(slot, b, *to)
    for e in (0, -1, 1, 2):
        for rel in (0, 1):
            for b in (0, 1):
                ex, ey = vec(e, b)
                for d in (-1, 1):
                    dx, dy = vec(d, 1 - b)
                    slot = at(ex + dx, rel, ey + dy)
                    arrived(slot, b)
                    if (rel == 0) == (d == -1):
                        fx, fy = vec(-d, 1 - b)
                        push(slot, b, fx, 0, fy)
    for e in (0, -1, 1, 2):
        for rel in (0, 1):
            for b in (0, 1):
                ex, ey = vec(e, b)
                dx, dy = vec(2, 1 - b)
                arrived(at(ex + dx, rel, ey + dy), b)
    mine.wait()

    found = jnp.zeros((NX * NZ * NY, share), F32)
    for k, peer in enumerate(peers_d):
        pltpu.make_async_copy(ids_ref, ids_all.at[peer], ids_recv.at[peer]).wait()
    per_owner = n_dp * share
    for k in range(n_dp):
        ids = ids_all[k]
        owner = ids // per_owner
        within = ids - owner * per_owner
        row = within - dp * share
        left = lax.broadcasted_iota(jnp.int32, (NX * NZ * NY, ids.shape[1]), 0) == owner
        right = lax.broadcasted_iota(jnp.int32, (share, ids.shape[1]), 0) == row
        found += mul(left.astype(F32).astype(BF16), right.astype(F32).astype(BF16), LANES)
    flat = lax.broadcasted_iota(jnp.int32, (NX * NZ * NY, n_rows), 1)
    slot_of = lax.broadcasted_iota(jnp.int32, (NX * NZ * NY, n_rows), 0)
    pick = (flat // share == slot_of).astype(F32)
    spread_out = mul(found, pick, (((0,), (0,)), ((), ())), lax.Precision.HIGHEST)
    row_of = lax.broadcasted_iota(jnp.int32, (share, n_rows), 0)
    row_flat = lax.broadcasted_iota(jnp.int32, (share, n_rows), 1)
    times_ref[...] = jnp.sum(jnp.where(row_flat % share == row_of, spread_out, 0.0), axis=0, keepdims=True)

    per = NZ * NY
    chunk = per * share
    tile = 256

    def features(slot, carry):
        s = rows[slot]
        here = pl.ds(pl.multiple_of(slot * share, share), share)
        f_hi[here, :width], f_lo[here, :width] = split(s)
        f_hi[here, width:], f_lo[here, width:] = split(s * s)
        return carry

    def plane(c):
        lax.fori_loop(c * per, (c + 1) * per, features, 0)
        cols = pl.ds(pl.multiple_of(c * chunk, chunk), chunk)

        def block(k, top):
            here = pl.ds(pl.multiple_of(k * tile, tile), tile)
            fh, fl = f_hi[cols, :], f_lo[cols, :]
            s = mul(a_hi[here, :], fh, LANES) + mul(a_hi[here, :], fl, LANES) + mul(a_lo[here, :], fh, LANES)
            s = s + offset[here, :]
            score[here, cols] = s
            return jnp.maximum(top, jnp.max(s, axis=0, keepdims=True))

        top = lax.fori_loop(0, comps // tile, block, jnp.full((1, chunk), -jnp.inf, F32))

        def raise_block(k, mass):
            here = pl.ds(pl.multiple_of(k * 64, 64), 64)
            e = jnp.exp(score[here, cols] - top)
            score[here, cols] = e
            return mass + jnp.sum(e, axis=0, keepdims=True)

        mass = lax.fori_loop(0, comps // 64, raise_block, jnp.zeros((1, chunk), F32))
        tops[:, cols] = top
        xb[x, :, cols] = top
        xb[x, :, pl.ds(pl.multiple_of(n_rows + c * chunk, chunk), chunk)] = mass

    for d in (0, -1, 1, 2):
        plane((x + d) % NX)

    logit_top = jnp.max(logits)
    logit_raised = jnp.exp(logits - logit_top)
    xb[x, :, pl.ds(2 * n_rows, 128)] = jnp.full((1, 128), logit_top, F32)
    xb[x, :, pl.ds(2 * n_rows + 128, 128)] = jnp.full((1, 128), jnp.sum(logit_raised), F32)

    def combine(ref, n):
        out = []
        for start, size in ((0, n_rows), (2 * n_rows, 128)):
            gap = n_rows if start == 0 else 128
            ts = [ref[k, :, start : start + size] for k in range(n)]
            ms = [ref[k, :, start + gap : start + gap + size] for k in range(n)]
            t = functools.reduce(jnp.maximum, ts)
            out.append((start, size, gap, t, sum(m * jnp.exp(a - t) for m, a in zip(ms, ts))))
        return out

    def fill(ref, index, results):
        for start, size, gap, t, m in results:
            ref[index, :, start : start + size] = t
            ref[index, :, start + gap : start + gap + size] = m

    def exchange(ref, index, peers, slots, s_sem, r_sem):
        copies = [
            send(ref.at[index], ref.at[index], s_sem.at[k], r_sem.at[index], comp=peer)
            for k, peer in enumerate(peers)
        ]
        for slot in slots:
            pltpu.make_async_copy(ref.at[slot], ref.at[slot], r_sem.at[slot]).wait()
        for copy in copies:
            copy.wait_send()

    exchange(xb, x, [at(d, 0, 0) for d in (1, 2, 3)], [(x + d) % NX for d in (1, 2, 3)], xs, xr)
    fill(yb, y, combine(xb, NX))
    exchange(yb, y, [at(0, 0, d) for d in (1, 2, 3)], [(y + d) % NY for d in (1, 2, 3)], ys, yr)
    fill(zb, zl, combine(yb, NY))
    exchange(zb, zl, [at(0, 1, 0)], [(zl + 1) % NZ], zs, zr)
    (_, _, _, peak, total), (_, _, _, logit_peak, logit_total) = combine(zb, NZ)
    factor = jnp.exp(tops[...] - peak) / total * times_ref[...]

    def responsibilities(k, carry):
        here = pl.ds(pl.multiple_of(k * row_block, row_block), row_block)
        r_hi[here, :], r_lo[here, :] = split(score[here, :] * factor)
        return carry

    lax.fori_loop(0, comps // row_block, responsibilities, 0)
    ones = jnp.ones((8, n_rows), BF16)
    mass_k = mul(ones, r_hi[...], LANES) + mul(ones, r_lo[...], LANES)
    counts_all[dp] = mass_k[0:1, :]
    count_copies = [
        send(counts_all.at[dp], counts_all.at[dp], cs.at[k], cr.at[dp], dp=peer)
        for k, peer in enumerate(peers_d)
    ]

    n_blocks = 2 * width // tile
    own_half = comps // NC
    q = own_half // NH
    side = tile // 2
    L, R = dp_at(-1, 0), dp_at(1, 0)
    sib = dp_at(0, 1)

    def moment(n, which):
        start = pl.multiple_of((n % 2) * width + (n // 2) * tile, tile)
        cols = pl.ds(start, tile)
        here = pl.ds(pl.multiple_of(which * own_half, own_half), own_half)
        fh, fl, rh = f_hi[:, cols], f_lo[:, cols], r_hi[here, :]
        return mul(rh, fh, INNER) + mul(rh, fl, INNER) + mul(r_lo[here, :], fh, INNER)

    def sib_copy(n):
        return pltpu.make_async_remote_copy(
            src_ref=sib_out.at[n], dst_ref=sib_in.at[n], send_sem=sib_s.at[n], recv_sem=sib_r.at[n],
            device_id={"dp": sib},
        )

    def for_sibling(n):
        sib_out[n] = moment(n, 1 - core)
        sib_copy(n).start()

    def chunk_of(n, o, b):
        return part.at[n, pl.ds(pl.multiple_of(o * q, q), q), pl.ds(b * side, side)]

    left_h, right_h, far_h = (h - 1) % NH, (h + 1) % NH, (h + 2) % NH

    def remote(src, dst, s, r, to):
        return Copy(src, dst, s, r, to)

    def cols_of(b):
        return pl.ds(b * side, side)

    def z_copies(n):
        return [
            remote(chunk_of(n, far_h, 0), from_r.at[n], opp_s.at[n, 0], opp_r.at[n, 0], L),
            remote(chunk_of(n, far_h, 1), from_l.at[n], opp_s.at[n, 1], opp_r.at[n, 1], R),
            remote(chunk_of(n, left_h, 1), own_r.at[n, :, cols_of(1)], dir_s.at[n, 0], dir_r.at[n, 0], L),
            remote(chunk_of(n, right_h, 0), own_l.at[n, :, cols_of(0)], dir_s.at[n, 1], dir_r.at[n, 1], R),
        ]

    def acc_copies(n):
        return [
            remote(chunk_of(n, left_h, 0), own_r.at[n, :, cols_of(0)], acc_s.at[n, 0], acc_r.at[n, 0], L),
            remote(chunk_of(n, right_h, 1), own_l.at[n, :, cols_of(1)], acc_s.at[n, 1], acc_r.at[n, 1], R),
        ]

    def relay(n):
        opp, acc = z_copies(n)[:2], acc_copies(n)
        opp[0].wait_recv()
        spot = chunk_of(n, left_h, 0)
        spot[...] = spot[...] + from_r[n]
        acc[0].start()
        opp[1].wait_recv()
        spot = chunk_of(n, right_h, 1)
        spot[...] = spot[...] + from_l[n]
        acc[1].start()

    for_sibling(0)

    def reduce_step(n, carry):
        @pl.when(n + 1 < n_blocks)
        def _():
            for_sibling(n + 1)

        own_block = moment(n, core)
        sib_copy(n).wait_recv()
        part[n] = own_block + sib_in[n]
        for copy in z_copies(n):
            copy.start()

        @pl.when(n > 0)
        def _():
            relay(n - 1)

        return carry

    lax.fori_loop(0, n_blocks, reduce_step, 0)
    relay(n_blocks - 1)

    for k, peer in enumerate(peers_d):
        pltpu.make_async_copy(counts_all.at[peer], counts_all.at[peer], cr.at[peer]).wait()
    counts = sum(counts_all[k] for k in range(n_dp))
    batch = 1.0 * n_dp * ids_ref.shape[1]
    index = jnp.full((1, comps), step_ref[0].astype(F32), F32)
    step = jnp.exp(-0.6 * jnp.log(2.0 + index / 8192.0))
    retain = 1.0 - step
    weights = logit_raised * (jnp.exp(logit_top - logit_peak[:, 0:1]) / logit_total[:, 0:1])
    prior = retain * weights
    mass_new = prior + step * counts / batch
    out_l[...] = jnp.log(mass_new)
    stacked = jnp.concatenate([mass_new, prior, counts, step, mass_new, prior, counts, step], axis=0)
    columns[...] = jnp.transpose(stacked)

    mine_at = pl.ds(pl.multiple_of(core * own_half + h * q, q), q)
    col = columns[mine_at, :]
    mass_c, prior_c, counts_c, step_c = (col[:, k : k + 1] for k in range(4))

    def reduced(n):
        z, acc = z_copies(n), acc_copies(n)
        for copy in (z[2], z[3], acc[0], acc[1]):
            copy.wait_recv()
        return part[n, pl.ds(pl.multiple_of(h * q, q), q), :] + own_r[n] + own_l[n]

    outs = (out_m, out_p)

    def out_piece(a, cb, o, c):
        here = pl.ds(pl.multiple_of(c * own_half + o * q, q), q)
        return outs[a].at[here, pl.ds(pl.multiple_of(cb * tile, tile), tile)]

    def z_gather(a, cb, o, s, r, to):
        return remote(out_piece(a, cb, o, core), out_piece(a, cb, o, core), s, r, to)

    def own_sends(cb):
        found = []
        for a in (0, 1):
            found.append(z_gather(a, cb, h, gz_s.at[cb, a, 0], gz_r.at[cb, a, 0], R))
            found.append(z_gather(a, cb, h, gz_s.at[cb, a, 1], gz_r.at[cb, a, 1], L))
            found.append(z_gather(a, cb, h, gs_s.at[cb, a, 0], gs_r.at[cb, a, 0], sib))
        return found

    def forwards(cb):
        return [
            z_gather(0, cb, left_h, gf_s.at[cb, 0], gz_r.at[cb, 0, 2], R),
            z_gather(1, cb, right_h, gf_s.at[cb, 1], gz_r.at[cb, 1, 2], L),
        ]

    def sib_sends(cb, a, k):
        o = (left_h, right_h, far_h)[k]
        return z_gather(a, cb, o, gs_s.at[cb, a, 1 + k], gs_r.at[cb, a, 1 + k], sib)

    def z_arrived(cb, a, k):
        o = (left_h, right_h, far_h)[k]
        ref = out_piece(a, cb, o, core)
        pltpu.make_async_copy(ref, ref, gz_r.at[cb, a, k]).wait()

    def update(cb, carry):
        first_m, second_m = reduced(2 * cb), reduced(2 * cb + 1)
        cols = pl.ds(pl.multiple_of(cb * tile, tile), tile)
        m, p = means_ref[mine_at, cols], prec_ref[mine_at, cols]
        new_m = (prior_c * m + step_c * first_m / batch) / mass_c
        moved = m - new_m
        spread = (
            prior_c * (1.0 / p + moved * moved)
            + step_c * (second_m - 2.0 * new_m * first_m + new_m * new_m * counts_c) / batch
        )
        out_m[mine_at, cols] = new_m
        out_p[mine_at, cols] = mass_c / spread
        for copy in own_sends(cb):
            copy.start()

        @pl.when(cb > 0)
        def _():
            pass_on(cb - 1)

        return carry

    def pass_on(cb):
        fwd = forwards(cb)
        z_arrived(cb, 0, 0)
        fwd[0].start()
        z_arrived(cb, 1, 1)
        fwd[1].start()
        sib_sends(cb, 0, 0).start()
        sib_sends(cb, 1, 1).start()
        z_arrived(cb, 1, 0)
        sib_sends(cb, 1, 0).start()
        z_arrived(cb, 0, 1)
        sib_sends(cb, 0, 1).start()

    n_cols = width // tile
    lax.fori_loop(0, n_cols, update, 0)
    pass_on(n_cols - 1)

    def finish(cb, carry):
        for a in (0, 1):
            z_arrived(cb, a, 2)
            sib_sends(cb, a, 2).start()
        return carry

    lax.fori_loop(0, n_cols, finish, 0)

    def drain(cb, carry):
        for copy in own_sends(cb) + forwards(cb):
            copy.wait_send()
        for a in (0, 1):
            for k in range(3):
                sib_sends(cb, a, k).wait_send()
            for k, o in enumerate((h, left_h, right_h, far_h)):
                ref = out_piece(a, cb, o, 1 - core)
                pltpu.make_async_copy(ref, ref, gs_r.at[cb, a, k]).wait()
        return carry

    lax.fori_loop(0, n_cols, drain, 0)

    def drain_reduce(n, carry):
        sib_copy(n).wait_send()
        for copy in z_copies(n) + acc_copies(n):
            copy.wait_send()
        return carry

    lax.fori_loop(0, n_blocks, drain_reduce, 0)
    for copy in waits + ids_copies + count_copies:
        copy.wait_send()


def local(row_ids, table, means, precisions, mix_logits, step_index):
    comps, width = means.shape
    n_comp, n_dp = lax.axis_size("comp"), lax.axis_size("dp")
    share = table.shape[0] // n_dp
    rows = share * n_comp
    n_ids = row_ids.shape[0]
    tile = 256
    blocks = 2 * width // tile
    n_cols = width // tile
    half = comps // NC
    q = half // NH
    packed = 2 * rows + 256
    vmem = pltpu.VMEM
    dma = pltpu.SemaphoreType.DMA
    space = pl.BlockSpec(memory_space=pltpu.VMEM)
    new_means, new_precisions, new_logits = pl.pallas_call(
        kernel,
        out_shape=(
            jax.ShapeDtypeStruct((comps, width), F32),
            jax.ShapeDtypeStruct((comps, width), F32),
            jax.ShapeDtypeStruct((1, comps), F32),
        ),
        in_specs=[space, pl.BlockSpec(memory_space=pl.ANY), space, space, space,
                  pl.BlockSpec(memory_space=pltpu.SMEM)],
        out_specs=(space, space, space),
        scratch_shapes=[
            vmem((n_comp, share, width), F32),
            vmem((n_dp, 1, n_ids), jnp.int32),
            vmem((comps, 2 * width), BF16),
            vmem((comps, 2 * width), BF16),
            vmem((rows, 2 * width), BF16),
            vmem((rows, 2 * width), BF16),
            vmem((comps, rows), F32),
            vmem((comps, rows), BF16),
            vmem((comps, rows), BF16),
            vmem((comps, 1), F32),
            vmem((1, rows), F32),
            vmem((1, rows), F32),
            vmem((NX, 1, packed), F32),
            vmem((NY, 1, packed), F32),
            vmem((NZ, 1, packed), F32),
            vmem((n_dp, 1, comps), F32),
            vmem((comps, 8), F32),
            vmem((blocks, half, tile), F32),
            vmem((blocks, half, tile), F32),
            vmem((blocks, half, tile), F32),
            vmem((blocks, q, tile // 2), F32),
            vmem((blocks, q, tile // 2), F32),
            vmem((blocks, q, tile), F32),
            vmem((blocks, q, tile), F32),
            dma((1,)), dma((n_dp,)), dma((n_dp,)), dma((64 + 8,)), dma((n_comp, 2)),
            dma((3,)), dma((NX,)), dma((3,)), dma((NY,)), dma((1,)), dma((NZ,)), dma((n_dp,)), dma((n_dp,)),
            dma((blocks,)), dma((blocks,)), dma((blocks, 2)), dma((blocks, 2)), dma((blocks, 2)),
            dma((blocks, 2)), dma((blocks, 2)), dma((blocks, 2)),
            dma((n_cols, 2, 2)), dma((n_cols, 2, 3)), dma((n_cols, 2)), dma((n_cols, 2, 4)), dma((n_cols, 2, 4)),
        ],
        compiler_params=pltpu.CompilerParams(
            collective_id=0, has_side_effects=True, vmem_limit_bytes=58 * 2**20
        ),
        name="em",
    )(row_ids.reshape(1, n_ids), table, means, precisions, mix_logits.reshape(1, comps), step_index)
    return new_means, new_precisions, new_logits.reshape(comps)


def solution(mesh):
    placed = (P("dp"), P("comp", None), P("comp", None), P("comp", None), P("comp"), P())
    return jax.shard_map(
        local,
        mesh=mesh,
        in_specs=placed,
        out_specs=(P("comp", None), P("comp", None), P("comp")),
        check_vma=False,
    )
```

time: 683 us -> 146 us (0.21)
  waiting for transfers between devices: 399 us -> 0 us
  blocking collectives: 196 us -> 0 us
  Pallas kernels: 0 us -> 139 us
  matrix products: 34.7 us -> 0 us
  other arithmetic: 26.9 us -> 0 us
  between operations: 14.8 us -> 1.3 us
    psum x2 -> x0, waiting for transfers between devices: 399 us -> none  [the longest x1 295 us: local(): samples = lax.psum(jnp.where(inside[:, None], picked, 0.0), 'comp')]
    pallas_call x0 -> x1, Pallas kernels: none -> 139 us  [local(): pl.pallas_call(kernel, out_shape=(jax.ShapeDtypeStruct((comps, width), F3...]
    psum x2 -> x0, blocking collectives: 129 us -> none  [the longest x1 65 us: local(): total_rows, total_logit = lax.psum((row_mass, logit_mass), 'comp')]
    pmax x1 -> x0, blocking collectives: 67.5 us -> none  [local(): peak_rows, peak_logit = lax.pmax((local_top, logit_top), 'comp')]
    dot_general x3 -> x0, matrix products: 34.7 us -> none  [the longest x1 14.8 us: local(): lax.dot_general(features, stacked, (((1,), (1,)), ((), ())), precision=hi...]
    reduce_sum x4 -> x0, other arithmetic: 9 us -> none  [the longest x1 3.51 us: local(): jnp.sum(jnp.log(precisions), axis=1)]
  transfers between devices with their start and end apart: 2 -> 0, of which waited for: 2 -> 0; matrix products, arithmetic and copies ran while one was open for 1% -> 0% of each run, Pallas kernels for 0% -> 0%
where the time goes in v2:
time: 146 us
  Pallas kernels  139 us (95%)
  local copies, waits for them, and re-layouts  5.21 us (4%)
    pallas_call x1, Pallas kernels, local(): pl.pallas_call(kernel, out_shape=(jax.ShapeDtypeStruct((comps, width), F3...  139 us
    unnamed x7, local copies, waits for them, and re-layouts  5.21 us

profile of v2, /device:TPU:33, one launch (start us, length us, event | category | flops | bytes accessed | tf_op | source)
XLA Modules:
  0.0 145.7 jit_solution(4058050525733573028)
XLA Ops:
  1.3 139.2 %em.1 = (f32[512,1024]{1,0:T(8,128)}, f32[512,1024]{1,0:T(8,128)}, f32[1,512]{1,0:T(1,128)}) custom-call(s32[1,1024]{1,0:T(1,128)} %bitcast.3, f32[256,1024]{1,0:T(8,128)} %table_ref.1, f32[512,1024]{1,0:T(8,128)} %means_ref.1, f32[512,1024]{1,0:T(8,128)} %prec_ref.1, f32[1,512]{1,0:T(1,128)} %bitcast.4, s32[1]{0:T(128)S(6)} %copy.12.step_ref), custom_call_target="tpu_custom_call" | custom-call | tf_op jit(solution)/shard_map/em/pallas_call | solution.py:518
  140.5 0.0 copy-start
  140.5 3.3 %copy.13 = f32[512,1024]{1,0:T(8,128)} copy(f32[512,1024]{1,0:T(8,128)} %get-tuple-element.12) | data formatting | bytes 4194304
  143.8 0.0 copy-done
  143.8 0.0 copy-start.1
  143.8 1.3 copy.14
  145.1 0.0 copy-done.1
  145.1 0.6 copy.15
Async XLA Ops:
  140.5 3.3 %copy-start = (f32[512,1024]{1,0:T(8,128)S(1)}, f32[512,1024]{1,0:T(8,128)}, u32[]{:S(2)}) copy-start(f32[512,1024]{1,0:T(8,128)} %get-tuple-element.13) | copy-start | bytes 6291460
  143.8 1.3 copy-start.1

commit v3 on v2

v3 whole, which is shorter than its diff:
```python
import functools

import jax
import jax.numpy as jnp
from jax import lax
from jax.experimental import pallas as pl
from jax.experimental.pallas import tpu as pltpu
from jax.sharding import PartitionSpec as P

F32, BF16 = jnp.float32, jnp.bfloat16
NX, NZ, NY = 4, 2, 4
NH, NC = 4, 2
ROUNDS = ((0, 24), (24, 8))
LANES = (((1,), (1,)), ((), ()))
INNER = (((1,), (0,)), ((), ()))


def split(value):
    high = value.astype(BF16)
    return high, (value - high.astype(F32)).astype(BF16)


def mul(left, right, dims, precision=None):
    return lax.dot_general(left, right, dims, precision=precision, preferred_element_type=F32)


class Copy:
    def __init__(self, src, dst, send_sem, recv_sem, to):
        self.make = lambda: pltpu.make_async_remote_copy(
            src_ref=src, dst_ref=dst, send_sem=send_sem, recv_sem=recv_sem, device_id={"dp": to}
        )

    def start(self):
        self.make().start()

    def wait_send(self):
        self.make().wait_send()

    def wait_recv(self):
        self.make().wait_recv()


def kernel(
    ids_ref, table_ref, means_hbm, prec_hbm, logits_ref, step_ref,
    out_m, out_p, out_mass,
    means_ref, prec_ref, stage, rows, ids_all, a_hi, a_lo, f_hi, f_lo, score, r_hi, r_lo, offset, tops, times_ref, counts_col,
    xb0, yb0, zb0, xb1, yb1, zb1, counts_all, columns,
    sib_out, sib_in, part, from_r, from_l, own_r, own_l,
    local_sem, ids_send, ids_recv, row_send, row_recv, xs, xr, ys, yr, zs, zr, cs, cr,
    sib_s, sib_r, opp_s, opp_r, dir_s, dir_r, acc_s, acc_r,
    gz_s, gz_r, gf_s, gs_s, gs_r, gl_s,
):
    dp, comp = lax.axis_index("dp"), lax.axis_index("comp")
    h, core = dp // NC, dp % NC
    x, zl, y = comp // (NZ * NY), (comp // NY) % NZ, comp % NY
    n_dp = NH * NC
    share = rows.shape[1]
    comps, width = means_ref.shape
    n_rows = f_hi.shape[0]

    def at(dx, dz, dy):
        return ((x + dx) % NX) * (NZ * NY) + ((zl + dz) % NZ) * NY + (y + dy) % NY

    def dp_at(dh, dc):
        return ((h + dh) % NH) * NC + (core + dc) % NC

    peers_c = [at(d, 0, 0) for d in (1, 2, 3)] + [at(0, 0, d) for d in (1, 2, 3)] + [at(0, 1, 0)]
    peers_d = [dp_at(a, b) for a in range(NH) for b in range(NC) if (a, b) != (0, 0)]
    for k, (src, dst) in enumerate(((means_hbm, means_ref), (prec_hbm, prec_ref))):
        pltpu.make_async_copy(src, dst, local_sem.at[1 + k]).start()
    barrier = pltpu.get_barrier_semaphore()
    for peer in peers_c:
        pl.semaphore_signal(barrier, inc=1, device_id={"comp": peer})
    for peer in peers_d:
        pl.semaphore_signal(barrier, inc=1, device_id={"dp": peer})
    pl.semaphore_wait(barrier, len(peers_c) + len(peers_d))

    waits = []

    def send(src, dst, send_sem, recv_sem, **where):
        copy = pltpu.make_async_remote_copy(
            src_ref=src, dst_ref=dst, send_sem=send_sem, recv_sem=recv_sem, device_id=where
        )
        copy.start()
        return copy

    me = at(0, 0, 0)
    mine = pltpu.make_async_copy(table_ref.at[pl.ds(dp * share, share)], rows.at[me], local_sem.at[0])
    mine.start()
    sends = [0]
    first = [(1, 0, 0), (-1, 0, 0)], [(0, 0, 1), (0, 0, -1)]
    wide = width // 2

    def piece(slot, b, t):
        off, size = ROUNDS[t]
        return rows.at[slot, pl.ds(off, size), pl.ds(b * wide, wide)]

    def push(slot, b, t, dx, dz, dy, source=None):
        src = piece(slot, b, t) if source is None else source
        k = sends[0]
        sends[0] += 1
        waits.append(
            send(src, piece(slot, b, t), row_send.at[k], row_recv.at[slot, b, t], comp=at(dx, dz, dy))
        )

    def arrived(slot, b, t):
        pltpu.make_async_copy(piece(slot, b, t), piece(slot, b, t), row_recv.at[slot, b, t]).wait()

    def vec(d, b):
        return (d, 0) if b == 0 else (0, d)

    def own(t):
        off, size = ROUNDS[t]
        src = [table_ref.at[pl.ds(dp * share + off, size), pl.ds(b * wide, wide)] for b in (0, 1)]
        for b in (0, 1):
            push(me, b, t, 0, 1, 0, src[b])
        for k in (0, 1):
            for b in (0, 1):
                for to in first[b ^ k]:
                    push(me, b, t, *to, src[b])

    def partner(t):
        slot = at(0, 1, 0)
        for b in (0, 1):
            arrived(slot, b, t)
            for to in first[b] + first[1 - b]:
                push(slot, b, t, *to)

    def first_near(t):
        for rel in (0, 1):
            for b in (0, 1):
                for d in (-1, 1):
                    dx, dy = vec(d, b)
                    slot = at(dx, rel, dy)
                    arrived(slot, b, t)
                    if (rel == 0) == (d == -1):
                        fx, fy = vec(-d, b)
                        push(slot, b, t, fx, 0, fy)
                    for to in first[1 - b]:
                        push(slot, b, t, *to)

    def first_far(t):
        for rel in (0, 1):
            for b in (0, 1):
                dx, dy = vec(2, b)
                slot = at(dx, rel, dy)
                arrived(slot, b, t)
                for to in first[1 - b]:
                    push(slot, b, t, *to)

    def second_near(t, e):
        for rel in (0, 1):
            for b in (0, 1):
                ex, ey = vec(e, b)
                for d in (-1, 1):
                    dx, dy = vec(d, 1 - b)
                    slot = at(ex + dx, rel, ey + dy)
                    arrived(slot, b, t)
                    if (rel == 0) == (d == -1):
                        fx, fy = vec(-d, 1 - b)
                        push(slot, b, t, fx, 0, fy)

    def second_far(t, e):
        for rel in (0, 1):
            for b in (0, 1):
                ex, ey = vec(e, b)
                dx, dy = vec(2, 1 - b)
                arrived(at(ex + dx, rel, ey + dy), b, t)

    own(0)
    own(1)
    ids_copies = [
        send(ids_ref, ids_all.at[dp], ids_send.at[k], ids_recv.at[dp], dp=peer)
        for k, peer in enumerate(peers_d)
    ]
    ids_all[dp] = ids_ref[...]

    row_block = 32

    def factors(i, carry):
        at_rows = pl.ds(pl.multiple_of(i * row_block, row_block), row_block)
        p, m = prec_ref[at_rows, :], means_ref[at_rows, :]
        cross = p * m
        hi, lo = split(cross)
        a_hi[at_rows, :width], a_lo[at_rows, :width] = hi, lo
        hi, lo = split(-0.5 * (p - 1.0))
        a_hi[at_rows, width:], a_lo[at_rows, width:] = hi, lo
        offset[at_rows, :] = 0.5 * jnp.sum(jnp.log(p) - cross * m, axis=1, keepdims=True)
        return carry

    n_factor = comps // row_block
    partner(0)
    for k, (src, dst) in enumerate(((means_hbm, means_ref), (prec_hbm, prec_ref))):
        pltpu.make_async_copy(src, dst, local_sem.at[1 + k]).wait()
    lax.fori_loop(0, n_factor // 4, factors, 0)
    first_near(0)
    lax.fori_loop(n_factor // 4, n_factor // 2, factors, 0)
    first_far(0)
    partner(1)
    second_near(0, 0)
    lax.fori_loop(n_factor // 2, n_factor, factors, 0)
    logits = logits_ref[...]
    turned = jnp.transpose(jnp.broadcast_to(logits, (8, comps)))
    offset[...] = offset[...] + turned[:, 0:1]
    second_near(0, -1)
    second_near(0, 1)
    first_near(1)

    owners = NX * NZ * NY
    found = jnp.zeros((owners, share), F32)
    for k, peer in enumerate(peers_d):
        pltpu.make_async_copy(ids_ref, ids_all.at[peer], ids_recv.at[peer]).wait()
    per_owner = n_dp * share
    for k in range(n_dp):
        ids = ids_all[k]
        owner = ids // per_owner
        row = ids - owner * per_owner - dp * share
        left = lax.broadcasted_iota(jnp.int32, (owners, ids.shape[1]), 0) == owner
        right = lax.broadcasted_iota(jnp.int32, (share, ids.shape[1]), 0) == row
        found += mul(left.astype(F32).astype(BF16), right.astype(F32).astype(BF16), LANES)
    bases = [owners * off for off, _ in ROUNDS]
    counted = [owners * size for _, size in ROUNDS]
    for (off, size), base, n in zip(ROUNDS, bases, counted):
        flat = lax.broadcasted_iota(jnp.int32, (owners, n), 1)
        pick = (flat // size == lax.broadcasted_iota(jnp.int32, (owners, n), 0)).astype(F32)
        spread_out = mul(found, pick, (((0,), (0,)), ((), ())), lax.Precision.HIGHEST)
        row_of = lax.broadcasted_iota(jnp.int32, (share, n), 0)
        row_flat = lax.broadcasted_iota(jnp.int32, (share, n), 1)
        times_ref[:, base : base + n] = jnp.sum(
            jnp.where(row_flat % size + off == row_of, spread_out, 0.0), axis=0, keepdims=True
        )

    second_near(0, 2)
    first_far(1)
    for e in (0, -1, 1, 2):
        second_far(0, e)
    mine.wait()

    chunk, tile = 256, 256
    packs = ((xb0, yb0, zb0), (xb1, yb1, zb1))

    def scores_of(t, c):
        base, n = bases[t], counted[t]
        cols = slice(base + c * chunk, base + (c + 1) * chunk)

        def block(k, top):
            here = pl.ds(pl.multiple_of(k * tile, tile), tile)
            fh, fl = f_hi[cols, :], f_lo[cols, :]
            s = mul(a_hi[here, :], fh, LANES) + mul(a_hi[here, :], fl, LANES) + mul(a_lo[here, :], fh, LANES)
            s = s + offset[here, :]
            score[here, cols] = s
            return jnp.maximum(top, jnp.max(s, axis=0, keepdims=True))

        top = lax.fori_loop(0, comps // tile, block, jnp.full((1, chunk), -jnp.inf, F32))

        def raise_block(k, mass):
            here = pl.ds(pl.multiple_of(k * 64, 64), 64)
            e = jnp.exp(score[here, cols] - top)
            score[here, cols] = e
            return mass + jnp.sum(e, axis=0, keepdims=True)

        mass = lax.fori_loop(0, comps // 64, raise_block, jnp.zeros((1, chunk), F32))
        tops[:, cols] = top
        packs[t][0][x, :, c * chunk : (c + 1) * chunk] = top
        packs[t][0][x, :, n + c * chunk : n + (c + 1) * chunk] = mass

    def features_of(t):
        off, size = ROUNDS[t]
        base, pair = bases[t], 2 * size

        def features(k, carry):
            s = jnp.concatenate([rows[2 * k, off : off + size, :], rows[2 * k + 1, off : off + size, :]], axis=0)
            here = pl.ds(pl.multiple_of(base + k * pair, 16), pair)
            f_hi[here, :width], f_lo[here, :width] = split(s)
            f_hi[here, width:], f_lo[here, width:] = split(s * s)
            return carry

        lax.fori_loop(0, owners // 2, features, 0)

    logit_top = jnp.max(logits)
    logit_raised = jnp.exp(logits - logit_top)

    def parts_of(t):
        n = counted[t]
        return ((0, n, n), (2 * n, 128, 128)) if t == 0 else ((0, n, n),)

    def combine(ref, n, t):
        out = []
        for start, size, gap in parts_of(t):
            ts = [ref[k, :, start : start + size] for k in range(n)]
            ms = [ref[k, :, start + gap : start + gap + size] for k in range(n)]
            top = functools.reduce(jnp.maximum, ts)
            out.append((start, size, gap, top, sum(m * jnp.exp(a - top) for m, a in zip(ms, ts))))
        return out

    def fill(ref, index, results):
        for start, size, gap, top, m in results:
            ref[index, :, start : start + size] = top
            ref[index, :, start + gap : start + gap + size] = m

    to_x, to_y, to_z = [at(d, 0, 0) for d in (1, 2, 3)], [at(0, 0, d) for d in (1, 2, 3)], [at(0, 1, 0)]
    from_x, from_y, from_z = [(x + d) % NX for d in (1, 2, 3)], [(y + d) % NY for d in (1, 2, 3)], [(zl + 1) % NZ]
    stages = ((x, to_x, from_x, xs, xr), (y, to_y, from_y, ys, yr), (zl, to_z, from_z, zs, zr))

    def stage_send(t, d):
        ref, (index, to, _, s_sem, r_sem) = packs[t][d], stages[d]
        for k, peer in enumerate(to):
            waits.append(send(ref.at[index], ref.at[index], s_sem.at[t, k], r_sem.at[t, index], comp=peer))

    def stage_wait(t, d):
        ref, (_, _, slots, _, r_sem) = packs[t][d], stages[d]
        for slot in slots:
            pltpu.make_async_copy(ref.at[slot], ref.at[slot], r_sem.at[t, slot]).wait()
        return combine(ref, (NX, NY, NZ)[d], t)

    def stage_next(t, d):
        fill(packs[t][d + 1], stages[d + 1][0], stage_wait(t, d))
        stage_send(t, d + 1)

    features_of(0)
    n_chunks = counted[0] // chunk
    for c in range(n_chunks):
        scores_of(0, c)
        if c == 0:
            second_near(1, 0)
            second_near(1, -1)
        elif c == 1:
            second_near(1, 1)
            second_near(1, 2)
    xb0[x, :, 2 * counted[0] : 2 * counted[0] + 128] = jnp.full((1, 128), logit_top, F32)
    xb0[x, :, 2 * counted[0] + 128 :] = jnp.full((1, 128), jnp.sum(logit_raised), F32)
    stage_send(0, 0)
    for e in (0, -1, 1, 2):
        second_far(1, e)
    features_of(1)
    stage_next(0, 0)
    scores_of(1, 0)
    stage_send(1, 0)
    stage_next(0, 1)

    def responsibilities(t, peak, total):
        cols = slice(bases[t], bases[t] + counted[t])
        factor = jnp.exp(tops[:, cols] - peak) / total * times_ref[:, cols]

        def one(k, carry):
            here = pl.ds(pl.multiple_of(k * row_block, row_block), row_block)
            r = score[here, cols] * factor
            r_hi[here, cols], r_lo[here, cols] = split(r)
            found = jnp.sum(r, axis=1, keepdims=True)
            counts_col[here, :] = found if t == 0 else counts_col[here, :] + found
            return carry

        lax.fori_loop(0, comps // row_block, one, 0)

    n_blocks = 2 * width // tile
    own_half = comps // NC
    q = own_half // NH
    side = tile // 2
    L, R = dp_at(-1, 0), dp_at(1, 0)
    sib = dp_at(0, 1)

    def moment(n, which, t):
        start = pl.multiple_of((n % 2) * width + (n // 2) * tile, tile)
        cols = pl.ds(start, tile)
        here = pl.ds(pl.multiple_of(which * own_half, own_half), own_half)
        deep = slice(bases[t], bases[t] + counted[t])
        fh, fl, rh = f_hi[deep, cols], f_lo[deep, cols], r_hi[here, deep]
        return mul(rh, fh, INNER) + mul(rh, fl, INNER) + mul(r_lo[here, deep], fh, INNER)

    def early(n, carry):
        sib_out[n] = moment(n, 1 - core, 0)
        part[n] = moment(n, core, 0)
        return carry

    (_, _, _, peak, total), (_, _, _, logit_peak, logit_total) = stage_wait(0, 2)
    responsibilities(0, peak, total)
    stage_next(1, 0)
    lax.fori_loop(0, n_blocks // 2, early, 0)
    stage_next(1, 1)
    lax.fori_loop(n_blocks // 2, n_blocks, early, 0)
    ((_, _, _, peak, total),) = stage_wait(1, 2)
    responsibilities(1, peak, total)

    def sib_copy(n):
        return Copy(sib_out.at[n], sib_in.at[n], sib_s.at[n], sib_r.at[n], sib)

    def for_sibling(n):
        sib_out[n] = sib_out[n] + moment(n, 1 - core, 1)
        sib_copy(n).start()

    def chunk_of(n, o, b):
        return part.at[n, pl.ds(pl.multiple_of(o * q, q), q), pl.ds(b * side, side)]

    left_h, right_h, far_h = (h - 1) % NH, (h + 1) % NH, (h + 2) % NH

    def remote(src, dst, s, r, to):
        return Copy(src, dst, s, r, to)

    def cols_of(b):
        return pl.ds(b * side, side)

    def z_copies(n):
        return [
            remote(chunk_of(n, far_h, 0), from_r.at[n], opp_s.at[n, 0], opp_r.at[n, 0], L),
            remote(chunk_of(n, far_h, 1), from_l.at[n], opp_s.at[n, 1], opp_r.at[n, 1], R),
            remote(chunk_of(n, left_h, 1), own_r.at[n, :, cols_of(1)], dir_s.at[n, 0], dir_r.at[n, 0], L),
            remote(chunk_of(n, right_h, 0), own_l.at[n, :, cols_of(0)], dir_s.at[n, 1], dir_r.at[n, 1], R),
        ]

    def acc_copies(n):
        return [
            remote(chunk_of(n, left_h, 0), own_r.at[n, :, cols_of(0)], acc_s.at[n, 0], acc_r.at[n, 0], L),
            remote(chunk_of(n, right_h, 1), own_l.at[n, :, cols_of(1)], acc_s.at[n, 1], acc_r.at[n, 1], R),
        ]

    def relay(n):
        opp, acc = z_copies(n)[:2], acc_copies(n)
        opp[0].wait_recv()
        spot = chunk_of(n, left_h, 0)
        spot[...] = spot[...] + from_r[n]
        acc[0].start()
        opp[1].wait_recv()
        spot = chunk_of(n, right_h, 1)
        spot[...] = spot[...] + from_l[n]
        acc[1].start()

    for_sibling(0)
    counts_all[dp] = jnp.transpose(jnp.broadcast_to(counts_col[...], (comps, 8)))[0:1, :]
    count_copies = [
        send(counts_all.at[dp], counts_all.at[dp], cs.at[k], cr.at[dp], dp=peer)
        for k, peer in enumerate(peers_d)
    ]

    def reduce_step(n, carry):
        @pl.when(n + 1 < n_blocks)
        def _():
            for_sibling(n + 1)

        own_block = part[n] + moment(n, core, 1)
        sib_copy(n).wait_recv()
        part[n] = own_block + sib_in[n]
        for copy in z_copies(n):
            copy.start()

        @pl.when(n > 0)
        def _():
            relay(n - 1)

        return carry

    lax.fori_loop(0, n_blocks, reduce_step, 0)
    relay(n_blocks - 1)

    for k, peer in enumerate(peers_d):
        pltpu.make_async_copy(counts_all.at[peer], counts_all.at[peer], cr.at[peer]).wait()
    counts = sum(counts_all[k] for k in range(n_dp))
    batch = 1.0 * n_dp * ids_ref.shape[1]
    index = jnp.full((1, comps), step_ref[0].astype(F32), F32)
    step = jnp.exp(-0.6 * jnp.log(2.0 + index / 8192.0))
    retain = 1.0 - step
    weights = logit_raised * (jnp.exp(logit_top - logit_peak[:, 0:1]) / logit_total[:, 0:1])
    prior = retain * weights
    mass_new = prior + step * counts / batch
    out_mass[...] = mass_new
    stacked = jnp.concatenate([mass_new, prior, counts, step, mass_new, prior, counts, step], axis=0)
    columns[...] = jnp.transpose(stacked)

    mine_at = pl.ds(pl.multiple_of(core * own_half + h * q, q), q)
    col = columns[mine_at, :]
    mass_c, prior_c, counts_c, step_c = (col[:, k : k + 1] for k in range(4))

    def reduced(n):
        z, acc = z_copies(n), acc_copies(n)
        for copy in (z[2], z[3], acc[0], acc[1]):
            copy.wait_recv()
        return part[n, pl.ds(pl.multiple_of(h * q, q), q), :] + own_r[n] + own_l[n]

    outs = (out_m, out_p)

    def out_piece(a, cb, o, c):
        here = pl.ds(pl.multiple_of(c * own_half + o * q, q), q)
        return outs[a].at[here, pl.ds(pl.multiple_of(cb * tile, tile), tile)]

    def own_piece(a, cb):
        return stage.at[a, :, pl.ds(pl.multiple_of(cb * tile, tile), tile)]

    def own_local(cb, a):
        return pltpu.make_async_copy(own_piece(a, cb), out_piece(a, cb, h, core), gl_s.at[cb, a])

    def z_gather(a, cb, o, s, r, to, src=None):
        src = out_piece(a, cb, o, core) if src is None else src
        return remote(src, out_piece(a, cb, o, core), s, r, to)

    def own_sends(cb):
        found = []
        for a in (0, 1):
            found.append(z_gather(a, cb, h, gz_s.at[cb, a, 0], gz_r.at[cb, a, 0], R, own_piece(a, cb)))
            found.append(z_gather(a, cb, h, gz_s.at[cb, a, 1], gz_r.at[cb, a, 1], L, own_piece(a, cb)))
            found.append(z_gather(a, cb, h, gs_s.at[cb, a, 0], gs_r.at[cb, a, 0], sib, own_piece(a, cb)))
        return found

    def forwards(cb):
        return [
            z_gather(0, cb, left_h, gf_s.at[cb, 0], gz_r.at[cb, 0, 2], R),
            z_gather(1, cb, right_h, gf_s.at[cb, 1], gz_r.at[cb, 1, 2], L),
        ]

    def sib_sends(cb, a, k):
        o = (left_h, right_h, far_h)[k]
        return z_gather(a, cb, o, gs_s.at[cb, a, 1 + k], gs_r.at[cb, a, 1 + k], sib)

    def z_arrived(cb, a, k):
        o = (left_h, right_h, far_h)[k]
        ref = out_piece(a, cb, o, core)
        pltpu.make_async_copy(ref, ref, gz_r.at[cb, a, k]).wait()

    def update(cb, carry):
        first_m, second_m = reduced(2 * cb), reduced(2 * cb + 1)
        cols = pl.ds(pl.multiple_of(cb * tile, tile), tile)
        m, p = means_ref[mine_at, cols], prec_ref[mine_at, cols]
        weighted = prior_c * m + step_c * first_m / batch
        new_m = weighted / mass_c
        moved = m - new_m
        spread = (
            prior_c * (1.0 / p + moved * moved)
            + step_c * (second_m - 2.0 * new_m * first_m + new_m * new_m * counts_c) / batch
        )
        stage[0, :, cols] = weighted
        stage[1, :, cols] = spread
        for copy in own_sends(cb):
            copy.start()
        for a in (0, 1):
            own_local(cb, a).start()

        @pl.when(cb > 0)
        def _():
            pass_on(cb - 1)

        return carry

    def pass_on(cb):
        fwd = forwards(cb)
        z_arrived(cb, 0, 0)
        fwd[0].start()
        z_arrived(cb, 1, 1)
        fwd[1].start()
        sib_sends(cb, 0, 0).start()
        sib_sends(cb, 1, 1).start()
        z_arrived(cb, 1, 0)
        sib_sends(cb, 1, 0).start()
        z_arrived(cb, 0, 1)
        sib_sends(cb, 0, 1).start()

    n_cols = width // tile
    lax.fori_loop(0, n_cols, update, 0)
    pass_on(n_cols - 1)

    def finish(cb, carry):
        for a in (0, 1):
            z_arrived(cb, a, 2)
            sib_sends(cb, a, 2).start()
        return carry

    lax.fori_loop(0, n_cols, finish, 0)

    def drain(cb, carry):
        for copy in own_sends(cb) + forwards(cb):
            copy.wait_send()
        for a in (0, 1):
            own_local(cb, a).wait()
            for k in range(3):
                sib_sends(cb, a, k).wait_send()
            for k, o in enumerate((h, left_h, right_h, far_h)):
                ref = out_piece(a, cb, o, 1 - core)
                pltpu.make_async_copy(ref, ref, gs_r.at[cb, a, k]).wait()
        return carry

    lax.fori_loop(0, n_cols, drain, 0)

    def drain_reduce(n, carry):
        sib_copy(n).wait_send()
        for copy in z_copies(n) + acc_copies(n):
            copy.wait_send()
        return carry

    lax.fori_loop(0, n_blocks, drain_reduce, 0)
    for copy in waits + ids_copies + count_copies:
        copy.wait_send()


def local(row_ids, table, means, precisions, mix_logits, step_index):
    comps, width = means.shape
    n_comp, n_dp = lax.axis_size("comp"), lax.axis_size("dp")
    share = table.shape[0] // n_dp
    rows = share * n_comp
    n_ids = row_ids.shape[0]
    tile = 256
    blocks = 2 * width // tile
    n_cols = width // tile
    half = comps // NC
    q = half // NH
    packed = [2 * n_comp * size + (256 if t == 0 else 0) for t, (_, size) in enumerate(ROUNDS)]
    anywhere = pl.BlockSpec(memory_space=pl.ANY)
    vmem = pltpu.VMEM
    dma = pltpu.SemaphoreType.DMA
    space = pl.BlockSpec(memory_space=pltpu.VMEM)
    weighted, spread, mass = pl.pallas_call(
        kernel,
        out_shape=(
            jax.ShapeDtypeStruct((comps, width), F32),
            jax.ShapeDtypeStruct((comps, width), F32),
            jax.ShapeDtypeStruct((1, comps), F32),
        ),
        in_specs=[space, anywhere, anywhere, anywhere, space, pl.BlockSpec(memory_space=pltpu.SMEM)],
        out_specs=(anywhere, anywhere, space),
        scratch_shapes=[
            vmem((comps, width), F32),
            vmem((comps, width), F32),
            vmem((2, q, width), F32),
            vmem((n_comp, share, width), F32),
            vmem((n_dp, 1, n_ids), jnp.int32),
            vmem((comps, 2 * width), BF16),
            vmem((comps, 2 * width), BF16),
            vmem((rows, 2 * width), BF16),
            vmem((rows, 2 * width), BF16),
            vmem((comps, rows), F32),
            vmem((comps, rows), BF16),
            vmem((comps, rows), BF16),
            vmem((comps, 1), F32),
            vmem((1, rows), F32),
            vmem((1, rows), F32),
            vmem((comps, 1), F32),
            *[vmem((n, 1, packed[t]), F32) for t in (0, 1) for n in (NX, NY, NZ)],
            vmem((n_dp, 1, comps), F32),
            vmem((comps, 8), F32),
            vmem((blocks, half, tile), F32),
            vmem((blocks, half, tile), F32),
            vmem((blocks, half, tile), F32),
            vmem((blocks, q, tile // 2), F32),
            vmem((blocks, q, tile // 2), F32),
            vmem((blocks, q, tile), F32),
            vmem((blocks, q, tile), F32),
            dma((3,)), dma((n_dp,)), dma((n_dp,)), dma((2 * 62,)), dma((n_comp, 2, 2)),
            dma((2, 3)), dma((2, NX)), dma((2, 3)), dma((2, NY)), dma((2, 1)), dma((2, NZ)), dma((n_dp,)), dma((n_dp,)),
            dma((blocks,)), dma((blocks,)), dma((blocks, 2)), dma((blocks, 2)), dma((blocks, 2)),
            dma((blocks, 2)), dma((blocks, 2)), dma((blocks, 2)),
            dma((n_cols, 2, 2)), dma((n_cols, 2, 3)), dma((n_cols, 2)), dma((n_cols, 2, 4)), dma((n_cols, 2, 4)), dma((n_cols, 2)),
        ],
        compiler_params=pltpu.CompilerParams(
            collective_id=0, has_side_effects=True, vmem_limit_bytes=58 * 2**20
        ),
        name="em",
    )(row_ids.reshape(1, n_ids), table, means, precisions, mix_logits.reshape(1, comps), step_index)
    mass = mass.reshape(comps)
    return weighted / mass[:, None], mass[:, None] / spread, jnp.log(mass)


def solution(mesh):
    placed = (P("dp"), P("comp", None), P("comp", None), P("comp", None), P("comp"), P())
    return jax.shard_map(
        local,
        mesh=mesh,
        in_specs=placed,
        out_specs=(P("comp", None), P("comp", None), P("comp")),
        check_vma=False,
    )
```

time: 146 us -> 148 us (1.014)
  other arithmetic: 0 us -> 4.73 us
  local copies, waits for them, and re-layouts: 5.21 us -> 0.59 us
  Pallas kernels: 139 us -> 141 us
    unnamed x7 -> x2, local copies, waits for them, and re-layouts: 5.21 us -> 0.01 us
    div x0 -> x1, other arithmetic: none -> 4.73 us  [local(): return (weighted / mass[:, None], mass[:, None] / spread, jnp.log(mass))]
    pallas_call x1, Pallas kernels: 139 us -> 141 us  [local(): pl.pallas_call(kernel, out_shape=(jax.ShapeDtypeStruct((comps, width), F3...]
where the time goes in v3:
time: 148 us; the launch traced here: 147 us
  Pallas kernels  141 us (95%)
  other arithmetic  4.73 us (3%)
    pallas_call x1, Pallas kernels, local(): pl.pallas_call(kernel, out_shape=(jax.ShapeDtypeStruct((comps, width), F3...  141 us
    div x1, other arithmetic, local(): return (weighted / mass[:, None], mass[:, None] / spread, jnp.log(mass))  4.73 us

profile of v3, /device:TPU:33, one launch (start us, length us, event | category | flops | bytes accessed | tf_op | source)
XLA Modules:
  0.0 147.5 jit_solution(17775853578066746265)
XLA Ops:
  1.3 140.9 %em.1 = (f32[512,1024]{1,0:T(8,128)}, f32[512,1024]{1,0:T(8,128)}, f32[1,512]{1,0:T(1,128)}) custom-call(s32[1,1024]{1,0:T(1,128)} %bitcast.5, f32[256,1024]{1,0:T(8,128)} %table_ref.1, f32[512,1024]{1,0:T(8,128)} %means_hbm.1, f32[512,1024]{1,0:T(8,128)} %prec_hbm.1, f32[1,512]{1,0:T(1,128)} %bitcast.6, s32[1]{0:T(128)S(6)} %copy.9.step_ref), custom_call_target="tpu_custom_call" | custom-call | tf_op jit(solution)/shard_map/em/pallas_call | solution.py:607
  142.2 0.0 copy-start
  142.2 4.7 %broadcast_divide_fusion = (f32[512,1024]{1,0:T(8,128)}, f32[512,1024]{1,0:T(8,128)}) fusion(f32[512,1024]{1,0:T(8,128)} %get-tuple-element.8, f32[512]{0:T(512)} %bitcast.3, f32[512,1024]{1,0:T(8,128)} %get-tuple-element.6), kind=kLoop, calls=%fused_computation | loop fusion | flops 1048576 | bytes 8390656 | tf_op jit(solution)/shard_map/div | solution.py:655
  146.9 0.0 copy-done
  146.9 0.6 log.3
Async XLA Ops:
  142.2 4.7 %copy-start = (f32[1,512]{1,0:T(1,128)S(1)}, f32[1,512]{1,0:T(1,128)}, u32[]{:S(2)}) copy-start(f32[1,512]{1,0:T(1,128)} %get-tuple-element.7) | copy-start | bytes 6148

commit v4 on v3

--- a/solution.py
+++ b/solution.py
@@ -10,7 +10,6 @@
 F32, BF16 = jnp.float32, jnp.bfloat16
 NX, NZ, NY = 4, 2, 4
 NH, NC = 4, 2
-ROUNDS = ((0, 24), (24, 8))
 LANES = (((1,), (1,)), ((), ()))
 INNER = (((1,), (0,)), ((), ()))
 
@@ -44,27 +43,34 @@
     ids_ref, table_ref, means_hbm, prec_hbm, logits_ref, step_ref,
     out_m, out_p, out_mass,
     means_ref, prec_ref, stage, rows, ids_all, a_hi, a_lo, f_hi, f_lo, score, r_hi, r_lo, offset, tops, times_ref, counts_col,
-    xb0, yb0, zb0, xb1, yb1, zb1, counts_all, columns,
+    xb, yb, peaks, scale, factors_ref, counts_all, columns,
     sib_out, sib_in, part, from_r, from_l, own_r, own_l,
-    local_sem, ids_send, ids_recv, row_send, row_recv, xs, xr, ys, yr, zs, zr, cs, cr,
+    local_sem, ids_send, ids_recv, row_send, row_recv, xs, xr, ys, yr, cs, cr,
     sib_s, sib_r, opp_s, opp_r, dir_s, dir_r, acc_s, acc_r,
     gz_s, gz_r, gf_s, gs_s, gs_r, gl_s,
 ):
     dp, comp = lax.axis_index("dp"), lax.axis_index("comp")
-    h, core = dp // NC, dp % NC
-    x, zl, y = comp // (NZ * NY), (comp // NY) % NZ, comp % NY
+    h, core = lax.div(dp, NC), lax.rem(dp, NC)
+    x, zl, y = lax.div(comp, NZ * NY), lax.rem(lax.div(comp, NY), NZ), lax.rem(comp, NY)
+    x_at = {d: lax.rem(x + (d % NX), NX) for d in (-1, 0, 1, 2, 3)}
+    y_at = {d: lax.rem(y + (d % NY), NY) for d in (-1, 0, 1, 2, 3)}
+    z_at = {0: zl, 1: 1 - zl}
+    h_at = {d: lax.rem(h + (d % NH), NH) for d in (-1, 0, 1, 2, 3)}
+    c_at = {0: core, 1: 1 - core}
     n_dp = NH * NC
     share = rows.shape[1]
     comps, width = means_ref.shape
     n_rows = f_hi.shape[0]
 
     def at(dx, dz, dy):
-        return ((x + dx) % NX) * (NZ * NY) + ((zl + dz) % NZ) * NY + (y + dy) % NY
+        return x_at[dx] * (NZ * NY) + z_at[dz] * NY + y_at[dy]
 
     def dp_at(dh, dc):
-        return ((h + dh) % NH) * NC + (core + dc) % NC
-
-    peers_c = [at(d, 0, 0) for d in (1, 2, 3)] + [at(0, 0, d) for d in (1, 2, 3)] + [at(0, 1, 0)]
+        return h_at[dh] * NC + c_at[dc]
+
+    plane = [(a, b) for a in range(NZ) for b in range(NY) if (a, b) != (0, 0)]
+    to_x, to_yz = [at(d, 0, 0) for d in (1, 2, 3)], [at(0, a, b) for a, b in plane]
+    peers_c = to_x + to_yz
     peers_d = [dp_at(a, b) for a in range(NH) for b in range(NC) if (a, b) != (0, 0)]
     for k, (src, dst) in enumerate(((means_hbm, means_ref), (prec_hbm, prec_ref))):
         pltpu.make_async_copy(src, dst, local_sem.at[1 + k]).start()
@@ -73,107 +79,6 @@
         pl.semaphore_signal(barrier, inc=1, device_id={"comp": peer})
     for peer in peers_d:
         pl.semaphore_signal(barrier, inc=1, device_id={"dp": peer})
-    pl.semaphore_wait(barrier, len(peers_c) + len(peers_d))
-
-    waits = []
-
-    def send(src, dst, send_sem, recv_sem, **where):
-        copy = pltpu.make_async_remote_copy(
-            src_ref=src, dst_ref=dst, send_sem=send_sem, recv_sem=recv_sem, device_id=where
-        )
-        copy.start()
-        return copy
-
-    me = at(0, 0, 0)
-    mine = pltpu.make_async_copy(table_ref.at[pl.ds(dp * share, share)], rows.at[me], local_sem.at[0])
-    mine.start()
-    sends = [0]
-    first = [(1, 0, 0), (-1, 0, 0)], [(0, 0, 1), (0, 0, -1)]
-    wide = width // 2
-
-    def piece(slot, b, t):
-        off, size = ROUNDS[t]
-        return rows.at[slot, pl.ds(off, size), pl.ds(b * wide, wide)]
-
-    def push(slot, b, t, dx, dz, dy, source=None):
-        src = piece(slot, b, t) if source is None else source
-        k = sends[0]
-        sends[0] += 1
-        waits.append(
-            send(src, piece(slot, b, t), row_send.at[k], row_recv.at[slot, b, t], comp=at(dx, dz, dy))
-        )
-
-    def arrived(slot, b, t):
-        pltpu.make_async_copy(piece(slot, b, t), piece(slot, b, t), row_recv.at[slot, b, t]).wait()
-
-    def vec(d, b):
-        return (d, 0) if b == 0 else (0, d)
-
-    def own(t):
-        off, size = ROUNDS[t]
-        src = [table_ref.at[pl.ds(dp * share + off, size), pl.ds(b * wide, wide)] for b in (0, 1)]
-        for b in (0, 1):
-            push(me, b, t, 0, 1, 0, src[b])
-        for k in (0, 1):
-            for b in (0, 1):
-                for to in first[b ^ k]:
-                    push(me, b, t, *to, src[b])
-
-    def partner(t):
-        slot = at(0, 1, 0)
-        for b in (0, 1):
-            arrived(slot, b, t)
-            for to in first[b] + first[1 - b]:
-                push(slot, b, t, *to)
-
-    def first_near(t):
-        for rel in (0, 1):
-            for b in (0, 1):
-                for d in (-1, 1):
-                    dx, dy = vec(d, b)
-                    slot = at(dx, rel, dy)
-                    arrived(slot, b, t)
-                    if (rel == 0) == (d == -1):
-                        fx, fy = vec(-d, b)
-                        push(slot, b, t, fx, 0, fy)
-                    for to in first[1 - b]:
-                        push(slot, b, t, *to)
-
-    def first_far(t):
-        for rel in (0, 1):
-            for b in (0, 1):
-                dx, dy = vec(2, b)
-                slot = at(dx, rel, dy)
-                arrived(slot, b, t)
-                for to in first[1 - b]:
-                    push(slot, b, t, *to)
-
-    def second_near(t, e):
-        for rel in (0, 1):
-            for b in (0, 1):
-                ex, ey = vec(e, b)
-                for d in (-1, 1):
-                    dx, dy = vec(d, 1 - b)
-                    slot = at(ex + dx, rel, ey + dy)
-                    arrived(slot, b, t)
-                    if (rel == 0) == (d == -1):
-                        fx, fy = vec(-d, 1 - b)
-                        push(slot, b, t, fx, 0, fy)
-
-    def second_far(t, e):
-        for rel in (0, 1):
-            for b in (0, 1):
-                ex, ey = vec(e, b)
-                dx, dy = vec(2, 1 - b)
-                arrived(at(ex + dx, rel, ey + dy), b, t)
-
-    own(0)
-    own(1)
-    ids_copies = [
-        send(ids_ref, ids_all.at[dp], ids_send.at[k], ids_recv.at[dp], dp=peer)
-        for k, peer in enumerate(peers_d)
-    ]
-    ids_all[dp] = ids_ref[...]
 
     row_block = 32
 
@@ -188,23 +93,115 @@
         offset[at_rows, :] = 0.5 * jnp.sum(jnp.log(p) - cross * m, axis=1, keepdims=True)
         return carry
 
-    n_factor = comps // row_block
-    partner(0)
     for k, (src, dst) in enumerate(((means_hbm, means_ref), (prec_hbm, prec_ref))):
         pltpu.make_async_copy(src, dst, local_sem.at[1 + k]).wait()
-    lax.fori_loop(0, n_factor // 4, factors, 0)
-    first_near(0)
-    lax.fori_loop(n_factor // 4, n_factor // 2, factors, 0)
-    first_far(0)
-    partner(1)
-    second_near(0, 0)
-    lax.fori_loop(n_factor // 2, n_factor, factors, 0)
+    lax.fori_loop(0, comps // row_block, factors, 0)
     logits = logits_ref[...]
     turned = jnp.transpose(jnp.broadcast_to(logits, (8, comps)))
     offset[...] = offset[...] + turned[:, 0:1]
-    second_near(0, -1)
-    second_near(0, 1)
-    first_near(1)
+    pl.semaphore_wait(barrier, len(peers_c) + len(peers_d))
+
+    waits = []
+
+    def send(src, dst, send_sem, recv_sem, **where):
+        copy = pltpu.make_async_remote_copy(
+            src_ref=src, dst_ref=dst, send_sem=send_sem, recv_sem=recv_sem, device_id=where
+        )
+        copy.start()
+        return copy
+
+    me = at(0, 0, 0)
+    mine = pltpu.make_async_copy(table_ref.at[pl.ds(dp * share, share)], rows.at[me], local_sem.at[0])
+    mine.start()
+    sends = [0]
+    first = [(1, 0, 0), (-1, 0, 0)], [(0, 0, 1), (0, 0, -1)]
+    half = share // 2
+
+    def piece(slot, b):
+        return rows.at[slot, pl.ds(b * half, half)]
+
+    def push(slot, b, dx, dz, dy, source=None):
+        src = piece(slot, b) if source is None else source
+        k = sends[0]
+        sends[0] += 1
+        waits.append(
+            send(src, piece(slot, b), row_send.at[k], row_recv.at[slot, b], comp=at(dx, dz, dy))
+        )
+
+    def arrived(slot, b):
+        pltpu.make_async_copy(piece(slot, b), piece(slot, b), row_recv.at[slot, b]).wait()
+
+    def vec(d, b):
+        return (d, 0) if b == 0 else (0, d)
+
+    def own():
+        src = [table_ref.at[pl.ds(dp * share + b * half, half)] for b in (0, 1)]
+        for b in (0, 1):
+            push(me, b, 0, 1, 0, src[b])
+        for k in (0, 1):
+            for b in (0, 1):
+                for to in first[b ^ k]:
+                    push(me, b, *to, src[b])
+
+    def partner():
+        slot = at(0, 1, 0)
+        for b in (0, 1):
+            arrived(slot, b)
+            for to in first[b] + first[1 - b]:
+                push(slot, b, *to)
+
+    def first_near():
+        for rel in (0, 1):
+            for b in (0, 1):
+                for d in (-1, 1):
+                    dx, dy = vec(d, b)
+                    slot = at(dx, rel, dy)
+                    arrived(slot, b)
+                    if (rel == 0) == (d == -1):
+                        fx, fy = vec(-d, b)
+                        push(slot, b, fx, 0, fy)
+                    for to in first[1 - b]:
+                        push(slot, b, *to)
+
+    def first_far():
+        for rel in (0, 1):
+            for b in (0, 1):
+                dx, dy = vec(2, b)
+                slot = at(dx, rel, dy)
+                arrived(slot, b)
+                for to in first[1 - b]:
+                    push(slot, b, *to)
+
+    def second_near(e):
+        for rel in (0, 1):
+            for b in (0, 1):
+                ex, ey = vec(e, b)
+                for d in (-1, 1):
+                    dx, dy = vec(d, 1 - b)
+                    slot = at(ex + dx, rel, ey + dy)
+                    arrived(slot, b)
+                    if (rel == 0) == (d == -1):
+                        fx, fy = vec(-d, 1 - b)
+                        push(slot, b, fx, 0, fy)
+
+    def second_far(e):
+        for rel in (0, 1):
+            for b in (0, 1):
+                ex, ey = vec(e, b)
+                dx, dy = vec(2, 1 - b)
+                arrived(at(ex + dx, rel, ey + dy), b)
+
+    own()
+    ids_copies = [
+        send(ids_ref, ids_all.at[dp], ids_send.at[k], ids_recv.at[dp], dp=peer)
+        for k, peer in enumerate(peers_d)
+    ]
+    ids_all[dp] = ids_ref[...]
+
+    partner()
+    first_near()
+    first_far()
+    second_near(0)
 
     owners = NX * NZ * NY
     found = jnp.zeros((owners, share), F32)
@@ -218,30 +215,47 @@
         left = lax.broadcasted_iota(jnp.int32, (owners, ids.shape[1]), 0) == owner
         right = lax.broadcasted_iota(jnp.int32, (share, ids.shape[1]), 0) == row
         found += mul(left.astype(F32).astype(BF16), right.astype(F32).astype(BF16), LANES)
-    bases = [owners * off for off, _ in ROUNDS]
-    counted = [owners * size for _, size in ROUNDS]
-    for (off, size), base, n in zip(ROUNDS, bases, counted):
-        flat = lax.broadcasted_iota(jnp.int32, (owners, n), 1)
-        pick = (flat // size == lax.broadcasted_iota(jnp.int32, (owners, n), 0)).astype(F32)
-        spread_out = mul(found, pick, (((0,), (0,)), ((), ())), lax.Precision.HIGHEST)
-        row_of = lax.broadcasted_iota(jnp.int32, (share, n), 0)
-        row_flat = lax.broadcasted_iota(jnp.int32, (share, n), 1)
-        times_ref[:, base : base + n] = jnp.sum(
-            jnp.where(row_flat % size + off == row_of, spread_out, 0.0), axis=0, keepdims=True
+    flat = lax.broadcasted_iota(jnp.int32, (owners, n_rows), 1)
+    slot_of = lax.broadcasted_iota(jnp.int32, (owners, n_rows), 0)
+    later = flat - owners * half
+    along_x = lax.div(flat, half)
+    xz = lax.rem(lax.div(later, half), NX * NZ)
+    along_y = xz * NY + lax.div(later, NX * NZ * half)
+    pick = (jnp.where(later < 0, along_x, along_y) == slot_of).astype(F32)
+    spread_out = mul(found, pick, (((0,), (0,)), ((), ())), lax.Precision.HIGHEST)
+    row_of = lax.broadcasted_iota(jnp.int32, (share, n_rows), 0)
+    row_flat = lax.broadcasted_iota(jnp.int32, (share, n_rows), 1)
+    row_flat = lax.rem(row_flat, half) + jnp.where(row_flat < owners * half, 0, half)
+    times_ref[...] = jnp.sum(jnp.where(row_flat == row_of, spread_out, 0.0), axis=0, keepdims=True)
+
+    tile = 256
+    block_cols = owners * half // NX
+    chunk = 2 * block_cols
+    order = (0, -1, 1, 2)
+
+    def places(e):
+        return (
+            pl.multiple_of(x_at[e] * block_cols, block_cols),
+            pl.multiple_of(owners * half + y_at[e] * block_cols, block_cols),
         )
 
-    second_near(0, 2)
-    first_far(1)
-    for e in (0, -1, 1, 2):
-        second_far(0, e)
-    mine.wait()
-
-    chunk, tile = 256, 256
-    packs = ((xb0, yb0, zb0), (xb1, yb1, zb1))
-
-    def scores_of(t, c):
-        base, n = bases[t], counted[t]
-        cols = slice(base + c * chunk, base + (c + 1) * chunk)
+    def features_of(e):
+        base = order.index(e) * chunk
+
+        def features(k, carry):
+            slots = (x_at[e] * (NZ * NY) + k, k * NY + y_at[e])
+            for b in (0, 1):
+                s = rows[slots[b], b * half : (b + 1) * half, :]
+                here = pl.ds(pl.multiple_of(base + b * block_cols + k * half, half), half)
+                f_hi[here, :width], f_lo[here, :width] = split(s)
+                f_hi[here, width:], f_lo[here, width:] = split(s * s)
+            return carry
+
+        lax.fori_loop(0, NZ * NY, features, 0)
+
+    def scores_of(e):
+        base = order.index(e) * chunk
+        cols = slice(base, base + chunk)
 
         def block(k, top):
             here = pl.ds(pl.multiple_of(k * tile, tile), tile)
@@ -261,32 +275,19 @@
 
         mass = lax.fori_loop(0, comps // 64, raise_block, jnp.zeros((1, chunk), F32))
         tops[:, cols] = top
-        packs[t][0][x, :, c * chunk : (c + 1) * chunk] = top
-        packs[t][0][x, :, n + c * chunk : n + (c + 1) * chunk] = mass
-
-    def features_of(t):
-        off, size = ROUNDS[t]
-        base, pair = bases[t], 2 * size
-
-        def features(k, carry):
-            s = jnp.concatenate([rows[2 * k, off : off + size, :], rows[2 * k + 1, off : off + size, :]], axis=0)
-            here = pl.ds(pl.multiple_of(base + k * pair, 16), pair)
-            f_hi[here, :width], f_lo[here, :width] = split(s)
-            f_hi[here, width:], f_lo[here, width:] = split(s * s)
-            return carry
-
-        lax.fori_loop(0, owners // 2, features, 0)
+        for b, place in enumerate(places(e)):
+            part_cols = slice(b * block_cols, (b + 1) * block_cols)
+            xb[x, :, pl.ds(place, block_cols)] = top[:, part_cols]
+            xb[x, :, pl.ds(pl.multiple_of(n_rows + place, block_cols), block_cols)] = mass[:, part_cols]
 
     logit_top = jnp.max(logits)
     logit_raised = jnp.exp(logits - logit_top)
 
-    def parts_of(t):
-        n = counted[t]
-        return ((0, n, n), (2 * n, 128, 128)) if t == 0 else ((0, n, n),)
-
-    def combine(ref, n, t):
+    parts = ((0, n_rows, n_rows), (2 * n_rows, 128, 128))
+
+    def combine(ref, n):
         out = []
-        for start, size, gap in parts_of(t):
+        for start, size, gap in parts:
             ts = [ref[k, :, start : start + size] for k in range(n)]
             ms = [ref[k, :, start + gap : start + gap + size] for k in range(n)]
             top = functools.reduce(jnp.maximum, ts)
@@ -298,59 +299,59 @@
             ref[index, :, start : start + size] = top
             ref[index, :, start + gap : start + gap + size] = m
 
-    to_x, to_y, to_z = [at(d, 0, 0) for d in (1, 2, 3)], [at(0, 0, d) for d in (1, 2, 3)], [at(0, 1, 0)]
-    from_x, from_y, from_z = [(x + d) % NX for d in (1, 2, 3)], [(y + d) % NY for d in (1, 2, 3)], [(zl + 1) % NZ]
-    stages = ((x, to_x, from_x, xs, xr), (y, to_y, from_y, ys, yr), (zl, to_z, from_z, zs, zr))
-
-    def stage_send(t, d):
-        ref, (index, to, _, s_sem, r_sem) = packs[t][d], stages[d]
+    from_x = [x_at[d] for d in (1, 2, 3)]
+    from_yz = [z_at[a] * NY + y_at[b] for a, b in plane]
+    stages = ((x, to_x, from_x, xs, xr), (zl * NY + y, to_yz, from_yz, ys, yr))
+
+    packs = (xb, yb)
+
+    def stage_send(d):
+        ref, (index, to, _, s_sem, r_sem) = packs[d], stages[d]
         for k, peer in enumerate(to):
-            waits.append(send(ref.at[index], ref.at[index], s_sem.at[t, k], r_sem.at[t, index], comp=peer))
-
-    def stage_wait(t, d):
-        ref, (_, _, slots, _, r_sem) = packs[t][d], stages[d]
+            waits.append(send(ref.at[index], ref.at[index], s_sem.at[k], r_sem.at[index], comp=peer))
+
+    def stage_wait(d):
+        ref, (_, _, slots, _, r_sem) = packs[d], stages[d]
         for slot in slots:
-            pltpu.make_async_copy(ref.at[slot], ref.at[slot], r_sem.at[t, slot]).wait()
-        return combine(ref, (NX, NY, NZ)[d], t)
-
-    def stage_next(t, d):
-        fill(packs[t][d + 1], stages[d + 1][0], stage_wait(t, d))
-        stage_send(t, d + 1)
-
+            pltpu.make_async_copy(ref.at[slot], ref.at[slot], r_sem.at[slot]).wait()
+        return combine(ref, (NX, NZ * NY)[d])
+
+    xb[x, :, 2 * n_rows : 2 * n_rows + 128] = jnp.full((1, 128), logit_top, F32)
+    xb[x, :, 2 * n_rows + 128 :] = jnp.full((1, 128), jnp.sum(logit_raised), F32)
+    second_near(-1)
+    second_far(0)
+    mine.wait()
     features_of(0)
-    n_chunks = counted[0] // chunk
-    for c in range(n_chunks):
-        scores_of(0, c)
-        if c == 0:
-            second_near(1, 0)
-            second_near(1, -1)
-        elif c == 1:
-            second_near(1, 1)
-            second_near(1, 2)
-    xb0[x, :, 2 * counted[0] : 2 * counted[0] + 128] = jnp.full((1, 128), logit_top, F32)
-    xb0[x, :, 2 * counted[0] + 128 :] = jnp.full((1, 128), jnp.sum(logit_raised), F32)
-    stage_send(0, 0)
-    for e in (0, -1, 1, 2):
-        second_far(1, e)
-    features_of(1)
-    stage_next(0, 0)
-    scores_of(1, 0)
-    stage_send(1, 0)
-    stage_next(0, 1)
-
-    def responsibilities(t, peak, total):
-        cols = slice(bases[t], bases[t] + counted[t])
-        factor = jnp.exp(tops[:, cols] - peak) / total * times_ref[:, cols]
-
+    scores_of(0)
+    second_near(1)
+    second_near(2)
+    for e in (-1, 1, 2):
+        second_far(e)
+        features_of(e)
+        scores_of(e)
+    stage_send(0)
+    fill(yb, stages[1][0], stage_wait(0))
+    stage_send(1)
+    (_, _, _, peak, total), (_, _, _, logit_peak, logit_total) = stage_wait(1)
+
+    peaks[...] = peak
+    scale[...] = times_ref[...] / total
+    for k, e in enumerate(order):
+        for b, place in enumerate(places(e)):
+            cols = slice(k * chunk + b * block_cols, k * chunk + (b + 1) * block_cols)
+            at_place = pl.ds(place, block_cols)
+            factors_ref[:, cols] = jnp.exp(tops[:, cols] - peaks[:, at_place]) * scale[:, at_place]
+    factor = factors_ref[...]
+
+    def responsibilities(which):
         def one(k, carry):
-            here = pl.ds(pl.multiple_of(k * row_block, row_block), row_block)
-            r = score[here, cols] * factor
-            r_hi[here, cols], r_lo[here, cols] = split(r)
-            found = jnp.sum(r, axis=1, keepdims=True)
-            counts_col[here, :] = found if t == 0 else counts_col[here, :] + found
+            here = pl.ds(pl.multiple_of(which * (comps // NC) + k * row_block, row_block), row_block)
+            r = score[here, :] * factor
+            r_hi[here, :], r_lo[here, :] = split(r)
+            counts_col[here, :] = jnp.sum(r, axis=1, keepdims=True)
             return carry
 
-        lax.fori_loop(0, comps // row_block, one, 0)
+        lax.fori_loop(0, comps // NC // row_block, one, 0)
 
     n_blocks = 2 * width // tile
     own_half = comps // NC
@@ -359,39 +360,24 @@
     L, R = dp_at(-1, 0), dp_at(1, 0)
     sib = dp_at(0, 1)
 
-    def moment(n, which, t):
-        start = pl.multiple_of((n % 2) * width + (n // 2) * tile, tile)
+    def moment(n, which):
+        start = pl.multiple_of(lax.rem(n, 2) * width + lax.div(n, 2) * tile, tile)
         cols = pl.ds(start, tile)
         here = pl.ds(pl.multiple_of(which * own_half, own_half), own_half)
-        deep = slice(bases[t], bases[t] + counted[t])
-        fh, fl, rh = f_hi[deep, cols], f_lo[deep, cols], r_hi[here, deep]
-        return mul(rh, fh, INNER) + mul(rh, fl, INNER) + mul(r_lo[here, deep], fh, INNER)
-
-    def early(n, carry):
-        sib_out[n] = moment(n, 1 - core, 0)
-        part[n] = moment(n, core, 0)
-        return carry
-
-    (_, _, _, peak, total), (_, _, _, logit_peak, logit_total) = stage_wait(0, 2)
-    responsibilities(0, peak, total)
-    stage_next(1, 0)
-    lax.fori_loop(0, n_blocks // 2, early, 0)
-    stage_next(1, 1)
-    lax.fori_loop(n_blocks // 2, n_blocks, early, 0)
-    ((_, _, _, peak, total),) = stage_wait(1, 2)
-    responsibilities(1, peak, total)
+        fh, fl, rh = f_hi[:, cols], f_lo[:, cols], r_hi[here, :]
+        return mul(rh, fh, INNER) + mul(rh, fl, INNER) + mul(r_lo[here, :], fh, INNER)
 
     def sib_copy(n):
         return Copy(sib_out.at[n], sib_in.at[n], sib_s.at[n], sib_r.at[n], sib)
 
     def for_sibling(n):
-        sib_out[n] = sib_out[n] + moment(n, 1 - core, 1)
+        sib_out[n] = moment(n, 1 - core)
         sib_copy(n).start()
 
     def chunk_of(n, o, b):
         return part.at[n, pl.ds(pl.multiple_of(o * q, q), q), pl.ds(b * side, side)]
 
-    left_h, right_h, far_h = (h - 1) % NH, (h + 1) % NH, (h + 2) % NH
+    left_h, right_h, far_h = h_at[-1], h_at[1], h_at[2]
 
     def remote(src, dst, s, r, to):
         return Copy(src, dst, s, r, to)
@@ -424,7 +410,9 @@
         spot[...] = spot[...] + from_l[n]
         acc[1].start()
 
+    responsibilities(1 - core)
     for_sibling(0)
+    responsibilities(core)
     counts_all[dp] = jnp.transpose(jnp.broadcast_to(counts_col[...], (comps, 8)))[0:1, :]
     count_copies = [
         send(counts_all.at[dp], counts_all.at[dp], cs.at[k], cr.at[dp], dp=peer)
@@ -436,7 +424,7 @@
         def _():
             for_sibling(n + 1)
 
-        own_block = part[n] + moment(n, core, 1)
+        own_block = moment(n, core)
         sib_copy(n).wait_recv()
         part[n] = own_block + sib_in[n]
         for copy in z_copies(n):
@@ -599,7 +587,7 @@
     n_cols = width // tile
     half = comps // NC
     q = half // NH
-    packed = [2 * n_comp * size + (256 if t == 0 else 0) for t, (_, size) in enumerate(ROUNDS)]
+    packed = 2 * rows + 256
     anywhere = pl.BlockSpec(memory_space=pl.ANY)
     vmem = pltpu.VMEM
     dma = pltpu.SemaphoreType.DMA
@@ -630,7 +618,11 @@
             vmem((1, rows), F32),
             vmem((1, rows), F32),
             vmem((comps, 1), F32),
-            *[vmem((n, 1, packed[t]), F32) for t in (0, 1) for n in (NX, NY, NZ)],
+            vmem((NX, 1, packed), F32),
+            vmem((NZ * NY, 1, packed), F32),
+            vmem((1, rows), F32),
+            vmem((1, rows), F32),
+            vmem((1, rows), F32),
             vmem((n_dp, 1, comps), F32),
             vmem((comps, 8), F32),
             vmem((blocks, half, tile), F32),
@@ -640,8 +632,8 @@
             vmem((blocks, q, tile // 2), F32),
             vmem((blocks, q, tile), F32),
             vmem((blocks, q, tile), F32),
-            dma((3,)), dma((n_dp,)), dma((n_dp,)), dma((2 * 62,)), dma((n_comp, 2, 2)),
-            dma((2, 3)), dma((2, NX)), dma((2, 3)), dma((2, NY)), dma((2, 1)), dma((2, NZ)), dma((n_dp,)), dma((n_dp,)),
+            dma((3,)), dma((n_dp,)), dma((n_dp,)), dma((62,)), dma((n_comp, 2)),
+            dma((NX - 1,)), dma((NX,)), dma((NZ * NY - 1,)), dma((NZ * NY,)), dma((n_dp,)), dma((n_dp,)),
             dma((blocks,)), dma((blocks,)), dma((blocks, 2)), dma((blocks, 2)), dma((blocks, 2)),
             dma((blocks, 2)), dma((blocks, 2)), dma((blocks, 2)),
             dma((n_cols, 2, 2)), dma((n_cols, 2, 3)), dma((n_cols, 2)), dma((n_cols, 2, 4)), dma((n_cols, 2, 4)), dma((n_cols, 2)),

time: 148 us -> 141 us (0.953); the launches traced: 147 us -> 138 us
  Pallas kernels: 141 us -> 131 us
    pallas_call x1, Pallas kernels: 141 us -> 131 us  [local(): pl.pallas_call(kernel, out_shape=(jax.ShapeDtypeStruct((comps, width), F3...]
where the time goes in v4:
time: 141 us; the launch traced here: 138 us
  Pallas kernels  131 us (93%)
  other arithmetic  4.73 us (3%)
    pallas_call x1, Pallas kernels, local(): pl.pallas_call(kernel, out_shape=(jax.ShapeDtypeStruct((comps, width), F3...  131 us
    div x1, other arithmetic, local(): return (weighted / mass[:, None], mass[:, None] / spread, jnp.log(mass))  4.73 us

profile of v4, /device:TPU:33, one launch (start us, length us, event | category | flops | bytes accessed | tf_op | source)
XLA Modules:
  0.0 138.1 jit_solution(6031674366780104081)
XLA Ops:
  1.3 131.5 %em.1 = (f32[512,1024]{1,0:T(8,128)}, f32[512,1024]{1,0:T(8,128)}, f32[1,512]{1,0:T(1,128)}) custom-call(s32[1,1024]{1,0:T(1,128)} %bitcast.5, f32[256,1024]{1,0:T(8,128)} %table_ref.1, f32[512,1024]{1,0:T(8,128)} %means_hbm.1, f32[512,1024]{1,0:T(8,128)} %prec_hbm.1, f32[1,512]{1,0:T(1,128)} %bitcast.6, s32[1]{0:T(128)S(6)} %copy.9.step_ref), custom_call_target="tpu_custom_call" | custom-call | tf_op jit(solution)/shard_map/em/pallas_call | solution.py:595
  132.8 0.0 copy-start
  132.8 4.7 %broadcast_divide_fusion = (f32[512,1024]{1,0:T(8,128)}, f32[512,1024]{1,0:T(8,128)}) fusion(f32[512,1024]{1,0:T(8,128)} %get-tuple-element.8, f32[512]{0:T(512)} %bitcast.3, f32[512,1024]{1,0:T(8,128)} %get-tuple-element.6), kind=kLoop, calls=%fused_computation | loop fusion | flops 1048576 | bytes 8390656 | tf_op jit(solution)/shard_map/div | solution.py:647
  137.5 0.0 copy-done
  137.5 0.6 log.3
Async XLA Ops:
  132.8 4.7 %copy-start = (f32[1,512]{1,0:T(1,128)S(1)}, f32[1,512]{1,0:T(1,128)}, u32[]{:S(2)}) copy-start(f32[1,512]{1,0:T(1,128)} %get-tuple-element.7) | copy-start | bytes 6148

commit v5 on v4

--- a/solution.py
+++ b/solution.py
@@ -319,16 +319,22 @@
     xb[x, :, 2 * n_rows : 2 * n_rows + 128] = jnp.full((1, 128), logit_top, F32)
     xb[x, :, 2 * n_rows + 128 :] = jnp.full((1, 128), jnp.sum(logit_raised), F32)
     second_near(-1)
+    second_near(1)
+    mine.wait()
     second_far(0)
-    mine.wait()
     features_of(0)
     scores_of(0)
-    second_near(1)
     second_near(2)
-    for e in (-1, 1, 2):
-        second_far(e)
-        features_of(e)
-        scores_of(e)
+    second_far(-1)
+    features_of(-1)
+    scores_of(-1)
+    second_far(1)
+    features_of(1)
+    scores_of(1)
+    second_far(2)
+    features_of(2)
+    scores_of(2)
+
     stage_send(0)
     fill(yb, stages[1][0], stage_wait(0))
     stage_send(1)
@@ -413,30 +419,31 @@
     responsibilities(1 - core)
     for_sibling(0)
     responsibilities(core)
+
+    def reduce_step(n, carry):
+        own_block = moment(n, core)
+        sib_copy(n).wait_recv()
+        part[n] = own_block + sib_in[n]
+        for copy in z_copies(n):
+            copy.start()
+
+        @pl.when(n + 1 < n_blocks)
+        def _():
+            for_sibling(n + 1)
+
+        @pl.when(n > 0)
+        def _():
+            relay(n - 1)
+
+        return carry
+
+    lax.fori_loop(0, 2, reduce_step, 0)
     counts_all[dp] = jnp.transpose(jnp.broadcast_to(counts_col[...], (comps, 8)))[0:1, :]
     count_copies = [
         send(counts_all.at[dp], counts_all.at[dp], cs.at[k], cr.at[dp], dp=peer)
         for k, peer in enumerate(peers_d)
     ]
-
-    def reduce_step(n, carry):
-        @pl.when(n + 1 < n_blocks)
-        def _():
-            for_sibling(n + 1)
-
-        own_block = moment(n, core)
-        sib_copy(n).wait_recv()
-        part[n] = own_block + sib_in[n]
-        for copy in z_copies(n):
-            copy.start()
-
-        @pl.when(n > 0)
-        def _():
-            relay(n - 1)
-
-        return carry
-
-    lax.fori_loop(0, n_blocks, reduce_step, 0)
+    lax.fori_loop(2, n_blocks, reduce_step, 0)
     relay(n_blocks - 1)
 
     for k, peer in enumerate(peers_d):
@@ -574,6 +581,14 @@
     lax.fori_loop(0, n_blocks, drain_reduce, 0)
     for copy in waits + ids_copies + count_copies:
         copy.wait_send()
+
+
+def finish_kernel(weighted_ref, spread_ref, mass_ref, means_out, precisions_out, logits_out):
+    mass = mass_ref[...]
+    column = jnp.transpose(jnp.broadcast_to(mass, (8, mass.shape[1])))[:, 0:1]
+    means_out[...] = weighted_ref[...] / column
+    precisions_out[...] = column / spread_ref[...]
+    logits_out[...] = jnp.log(mass)
 
 
 def local(row_ids, table, means, precisions, mix_logits, step_index):
@@ -643,8 +658,22 @@
         ),
         name="em",
     )(row_ids.reshape(1, n_ids), table, means, precisions, mix_logits.reshape(1, comps), step_index)
-    mass = mass.reshape(comps)
-    return weighted / mass[:, None], mass[:, None] / spread, jnp.log(mass)
+    rows_at_once = 128
+    wide = pl.BlockSpec((rows_at_once, width), lambda i: (i, 0))
+    thin = pl.BlockSpec((1, rows_at_once), lambda i: (0, i))
+    new_means, new_precisions, new_logits = pl.pallas_call(
+        finish_kernel,
+        grid=(comps // rows_at_once,),
+        out_shape=(
+            jax.ShapeDtypeStruct((comps, width), F32),
+            jax.ShapeDtypeStruct((comps, width), F32),
+            jax.ShapeDtypeStruct((1, comps), F32),
+        ),
+        in_specs=[wide, wide, thin],
+        out_specs=(wide, wide, thin),
+        name="finish",
+    )(weighted, spread, mass)
+    return new_means, new_precisions, new_logits.reshape(comps)
 
 
 def solution(mesh):

time: 141 us -> 138 us (0.979); the launches traced: 138 us -> 138 us
  Pallas kernels: 131 us -> 137 us
  other arithmetic: 4.73 us -> 0 us
    pallas_call x0 -> x1, Pallas kernels: none -> 4.94 us  [local(): pl.pallas_call(finish_kernel, grid=(comps // rows_at_once,), out_shape=(j...]
    div x1 -> x0, other arithmetic: 4.73 us -> none  [local(): return (weighted / mass[:, None], mass[:, None] / spread, jnp.log(mass))]
where the time goes in v5:
time: 138 us
  Pallas kernels  137 us (99%)
    pallas_call x1, Pallas kernels, local(): pl.pallas_call(kernel, out_shape=(jax.ShapeDtypeStruct((comps, width), F3...  132 us
    pallas_call x1, Pallas kernels, local(): pl.pallas_call(finish_kernel, grid=(comps // rows_at_once,), out_shape=(j...  4.94 us

profile of v5, /device:TPU:33, one launch (start us, length us, event | category | flops | bytes accessed | tf_op | source)
XLA Modules:
  0.0 138.2 jit_solution(15602002924081864686)
XLA Ops:
  1.3 132.0 %em.1 = (f32[512,1024]{1,0:T(8,128)}, f32[512,1024]{1,0:T(8,128)}, f32[1,512]{1,0:T(1,128)}) custom-call(s32[1,1024]{1,0:T(1,128)} %bitcast.3, f32[256,1024]{1,0:T(8,128)} %table_ref.1, f32[512,1024]{1,0:T(8,128)} %means_hbm.1, f32[512,1024]{1,0:T(8,128)} %prec_hbm.1, f32[1,512]{1,0:T(1,128)} %bitcast.4, s32[1]{0:T(128)S(6)} %copy.9.step_ref), custom_call_target="tpu_custom_call" | custom-call | tf_op jit(solution)/shard_map/em/pallas_call | solution.py:610
  133.2 4.9 %finish.1 = (f32[512,1024]{1,0:T(8,128)}, f32[512,1024]{1,0:T(8,128)}, f32[1,512]{1,0:T(1,128)}) custom-call(f32[512,1024]{1,0:T(8,128)} %get-tuple-element.9.weighted_ref, f32[512,1024]{1,0:T(8,128)} %get-tuple-element.10.spread_ref, f32[1,512]{1,0:T(1,128)} %get-tuple-element.11.mass_ref), custom_call_target="tpu_custom_call" | custom-call | tf_op jit(solution)/shard_map/finish/pallas_call | solution.py:664

commit v6 on v5

--- a/solution.py
+++ b/solution.py
@@ -658,7 +658,7 @@
         ),
         name="em",
     )(row_ids.reshape(1, n_ids), table, means, precisions, mix_logits.reshape(1, comps), step_index)
-    rows_at_once = 128
+    rows_at_once = 256
     wide = pl.BlockSpec((rows_at_once, width), lambda i: (i, 0))
     thin = pl.BlockSpec((1, rows_at_once), lambda i: (0, i))
     new_means, new_precisions, new_logits = pl.pallas_call(

time: 138 us -> 137 us (level)
  no operation moved by 1% of the time
where the time goes in v6:
time: 137 us
  Pallas kernels  136 us (99%)
    pallas_call x1, Pallas kernels, local(): pl.pallas_call(kernel, out_shape=(jax.ShapeDtypeStruct((comps, width), F3...  132 us
    pallas_call x1, Pallas kernels, local(): pl.pallas_call(finish_kernel, grid=(comps // rows_at_once,), out_shape=(j...  3.9 us

profile of v6, /device:TPU:33, one launch (start us, length us, event | category | flops | bytes accessed | tf_op | source)
XLA Modules:
  0.0 137.1 jit_solution(16674024088701585220)
XLA Ops:
  1.3 132.0 %em.1 = (f32[512,1024]{1,0:T(8,128)}, f32[512,1024]{1,0:T(8,128)}, f32[1,512]{1,0:T(1,128)}) custom-call(s32[1,1024]{1,0:T(1,128)} %bitcast.3, f32[256,1024]{1,0:T(8,128)} %table_ref.1, f32[512,1024]{1,0:T(8,128)} %means_hbm.1, f32[512,1024]{1,0:T(8,128)} %prec_hbm.1, f32[1,512]{1,0:T(1,128)} %bitcast.4, s32[1]{0:T(128)S(6)} %copy.9.step_ref), custom_call_target="tpu_custom_call" | custom-call | tf_op jit(solution)/shard_map/em/pallas_call | solution.py:610
  133.2 3.9 %finish.1 = (f32[512,1024]{1,0:T(8,128)}, f32[512,1024]{1,0:T(8,128)}, f32[1,512]{1,0:T(1,128)}) custom-call(f32[512,1024]{1,0:T(8,128)} %get-tuple-element.9.weighted_ref, f32[512,1024]{1,0:T(8,128)} %get-tuple-element.10.spread_ref, f32[1,512]{1,0:T(1,128)} %get-tuple-element.11.mass_ref), custom_call_target="tpu_custom_call" | custom-call | tf_op jit(solution)/shard_map/finish/pallas_call | solution.py:664
